TPU v7x, 8 devices: a whole 2x2x1 slice. The times are simulated.
8 devices in a mesh: dp: 1 (over z), pp: 2 (over y), ep: 4 (over x, core).
Axes of the slice: x: 2, y: 2, z: 1, core: 2. Of those that a mesh axis runs over, the one named last changes fastest.
Arguments:
- hidden_in: bfloat16 [64, 128, 1024], P(None, ('dp', 'ep'))
- seq_pos: int32 [64, 128], P(None, ('dp', 'ep'))
- k_cache: bfloat16 [2, 64, 128, 16, 8, 64], P('pp', None, ('dp', 'ep'))
- v_cache: bfloat16 [2, 64, 128, 16, 8, 64], P('pp', None, ('dp', 'ep'))
- expert_ids: int32 [2, 64, 128, 8], P('pp', None, ('dp', 'ep'))
- w_query: bfloat16 [2, 1024, 1024], P('pp')
- w_key: bfloat16 [2, 1024, 512], P('pp')
- w_value: bfloat16 [2, 1024, 512], P('pp')
- w_out: bfloat16 [2, 1024, 1024], P('pp')
- attn_gain: bfloat16 [2, 1024], P('pp')
- mlp_gain: bfloat16 [2, 1024], P('pp')
- w_router: bfloat16 [2, 1024, 32], P('pp')
- w_gate: bfloat16 [2, 32, 1024, 512], P('pp', 'ep')
- w_up: bfloat16 [2, 32, 1024, 512], P('pp', 'ep')
- w_down: bfloat16 [2, 32, 512, 1024], P('pp', 'ep')
- final_gain: bfloat16 [1024], replicated
Outputs:
- output 1: bfloat16 [64, 128, 1024], P(None, ('dp', 'ep'))
- output 2: bfloat16 [2, 64, 128, 8, 64], P('pp', None, ('dp', 'ep'))
- output 3: bfloat16 [2, 64, 128, 8, 64], P('pp', None, ('dp', 'ep'))
All inputs are finite; a program needn't handle non-finite values.
Results may differ from a plain program's by a relative error of at most 0.0174593.
Values are sent between devices in bfloat16 or wider.
A program may use at most 1 GiB of HBM per device.

v0:
```python
import jax
import jax.numpy as jnp
from jax import lax
from jax.sharding import PartitionSpec as P

THETA = 1000000.0
EPS = 1e-05


def rms_norm(in_vals, gain_vec):
    vals_f32 = in_vals.astype(jnp.float32)
    inv_rms = lax.rsqrt(jnp.mean(vals_f32 * vals_f32, axis=-1, keepdims=True) + EPS)
    return (vals_f32 * inv_rms * gain_vec.astype(jnp.float32)).astype(jnp.bfloat16)


def rotate(head_vecs, positions):
    half_dim = head_vecs.shape[-1] // 2
    inv_freq = THETA ** (-jnp.arange(half_dim, dtype=jnp.float32) / half_dim)
    angles = positions.astype(jnp.float32)[:, None, None] * inv_freq
    cos_ang = jnp.cos(angles)
    sin_ang = jnp.sin(angles)
    first_half = head_vecs[..., :half_dim].astype(jnp.float32)
    second_half = head_vecs[..., half_dim:].astype(jnp.float32)
    return jnp.concatenate([first_half * cos_ang - second_half * sin_ang, second_half * cos_ang + first_half * sin_ang], axis=-1).astype(jnp.bfloat16)


def attend(q_heads, key_new, val_new, k_rows, v_rows, positions):
    tokens, kv_heads, head_dim = key_new.shape
    ctx_len = k_rows.shape[1]
    q_groups = q_heads.reshape(tokens, kv_heads, -1, head_dim)
    score_scale = head_dim ** -0.5
    cache_scores = jnp.einsum("bkgh,btkh->bkgt", q_groups, k_rows, preferred_element_type=jnp.float32) * score_scale
    is_valid = jnp.arange(ctx_len)[None, None, None, :] < positions[:, None, None, None]
    cache_scores = jnp.where(is_valid, cache_scores, -jnp.inf)
    self_score = jnp.einsum("bkgh,bkh->bkg", q_groups, key_new, preferred_element_type=jnp.float32)[..., None] * score_scale
    top_score = jnp.maximum(jnp.max(cache_scores, axis=-1, keepdims=True), self_score)
    cache_w = jnp.exp(cache_scores - top_score)
    self_w = jnp.exp(self_score - top_score)
    weight_sum = jnp.sum(cache_w, axis=-1, keepdims=True) + self_w
    cache_w = (cache_w / weight_sum).astype(jnp.bfloat16)
    self_w = (self_w / weight_sum).astype(jnp.bfloat16)
    attn_out = jnp.einsum("bkgt,btkh->bkgh", cache_w, v_rows, preferred_element_type=jnp.float32) + self_w.astype(jnp.float32) * val_new.astype(jnp.float32)[:, :, None, :]
    return attn_out.astype(jnp.bfloat16).reshape(tokens, -1)


def attn_block(hidden, positions, k_rows, v_rows, w_q, w_k, w_v, w_o, gain_vec):
    tokens = hidden.shape[0]
    kv_heads, head_dim = k_rows.shape[2], k_rows.shape[3]
    normed = rms_norm(hidden, gain_vec)
    q_heads = jnp.dot(normed, w_q, preferred_element_type=jnp.float32).astype(jnp.bfloat16).reshape(tokens, -1, head_dim)
    key_new = jnp.dot(normed, w_k, preferred_element_type=jnp.float32).astype(jnp.bfloat16).reshape(tokens, kv_heads, head_dim)
    val_new = jnp.dot(normed, w_v, preferred_element_type=jnp.float32).astype(jnp.bfloat16).reshape(tokens, kv_heads, head_dim)
    q_heads = rotate(q_heads, positions)
    key_new = rotate(key_new, positions)
    attn_out = attend(q_heads, key_new, val_new, k_rows, v_rows, positions)
    hidden = (hidden.astype(jnp.float32) + jnp.dot(attn_out, w_o, preferred_element_type=jnp.float32)).astype(jnp.bfloat16)
    return hidden, key_new, val_new


def row_capacity(tokens, top_k, ep_size):
    return tokens // 2 * ((top_k + ep_size - 1) // ep_size) + tokens * top_k // (2 * ep_size)


def expert_rows(in_rows, labels, gate_col, w_g, w_u, w_d):
    local_count = w_g.shape[0]
    sort_order = jnp.argsort(labels, stable=True)
    group_sizes = jnp.sum(labels[:, None] == jnp.arange(local_count)[None, :], axis=0).astype(jnp.int32)
    sorted_rows = in_rows[sort_order]
    gate_h = lax.ragged_dot(sorted_rows, w_g, group_sizes, preferred_element_type=jnp.float32)
    up_h = lax.ragged_dot(sorted_rows, w_u, group_sizes, preferred_element_type=jnp.float32)
    act_rows = (jax.nn.silu(gate_h) * up_h).astype(jnp.bfloat16)
    down_h = lax.ragged_dot(act_rows, w_d, group_sizes, preferred_element_type=jnp.float32)
    in_group = (labels < local_count)[sort_order]
    weighted = jnp.where(in_group[:, None], gate_col[sort_order][:, None] * down_h, 0.0).astype(jnp.bfloat16)
    return weighted[jnp.argsort(sort_order)]


def moe_routed(normed, choice_ids, gate_vals, w_g, w_u, w_d, ep_size):
    tokens, top_k = choice_ids.shape
    local_count = w_g.shape[0]
    capacity = row_capacity(tokens, top_k, ep_size)
    flat_ids = choice_ids.reshape(-1)
    dest_dev = flat_ids // local_count
    onehot_dev = (dest_dev[:, None] == jnp.arange(ep_size)[None, :]).astype(jnp.int32)
    dest_rank = jnp.sum((jnp.cumsum(onehot_dev, axis=0) - onehot_dev) * onehot_dev, axis=1)
    buf_pos = dest_dev * capacity + dest_rank
    filler = jnp.zeros((ep_size * capacity,), jnp.int32).at[buf_pos].set(jnp.arange(flat_ids.shape[0], dtype=jnp.int32) + 1)
    occupied = filler > 0
    src_slot = jnp.maximum(filler - 1, 0)
    send_rows = jnp.where(occupied[:, None], normed[src_slot // top_k], jnp.zeros((), jnp.bfloat16))
    send_gate = jnp.where(occupied, gate_vals.reshape(-1)[src_slot], 0.0)
    send_label = jnp.where(occupied, flat_ids[src_slot] % local_count, local_count).astype(jnp.float32)
    send_meta = jnp.stack([send_gate, send_label], axis=1)
    recv_rows = lax.all_to_all(send_rows, "ep", 0, 0, tiled=True)
    recv_meta = lax.all_to_all(send_meta, "ep", 0, 0, tiled=True)
    weighted = expert_rows(recv_rows, recv_meta[:, 1].astype(jnp.int32), recv_meta[:, 0], w_g, w_u, w_d)
    back_rows = lax.all_to_all(weighted, "ep", 0, 0, tiled=True)
    per_slot = back_rows[buf_pos].astype(jnp.float32).reshape(tokens, top_k, -1)
    return jnp.sum(per_slot, axis=1).astype(jnp.bfloat16)


def solution(mesh):
    ep_size = mesh.shape["ep"]
    stage_count = mesh.shape["pp"]
    rows_spec = ("dp", "ep")
    three_dim = P("pp", None, None)
    two_dim = P("pp", None)
    expert_spec = P("pp", "ep", None, None)
    cache_spec = P("pp", None, rows_spec, None, None, None)
    new_spec = P("pp", None, rows_spec, None, None)
    in_specs = (P(None, rows_spec, None), P(None, rows_spec), cache_spec, cache_spec, P("pp", None, rows_spec, None), three_dim, three_dim, three_dim, three_dim, two_dim, two_dim, three_dim, expert_spec, expert_spec, expert_spec, P(None))
    out_specs = (P(None, rows_spec, None), new_spec, new_spec)
    shift_perm = [(src_stage, src_stage + 1) for src_stage in range(stage_count - 1)]

    def device_fn(hidden_in, seq_pos, k_cache, v_cache, expert_ids, w_query, w_key, w_value, w_out, attn_gain, mlp_gain, w_router, w_gate, w_up, w_down, final_gain):
        stage_idx = lax.axis_index("pp")
        micro_count = hidden_in.shape[0]
        layer_count = w_query.shape[0]

        def run_stage(stage_in, micro_idx):
            positions = lax.dynamic_index_in_dim(seq_pos, micro_idx, 0, keepdims=False)
            hidden = stage_in
            k_list = []
            v_list = []
            for layer_idx in range(layer_count):
                k_rows = lax.dynamic_index_in_dim(k_cache[layer_idx], micro_idx, 0, keepdims=False)
                v_rows = lax.dynamic_index_in_dim(v_cache[layer_idx], micro_idx, 0, keepdims=False)
                hidden, key_new, val_new = attn_block(hidden, positions, k_rows, v_rows, w_query[layer_idx], w_key[layer_idx], w_value[layer_idx], w_out[layer_idx], attn_gain[layer_idx])
                choice_ids = lax.dynamic_index_in_dim(expert_ids[layer_idx], micro_idx, 0, keepdims=False)
                normed = rms_norm(hidden, mlp_gain[layer_idx])
                logits = jnp.dot(normed, w_router[layer_idx], preferred_element_type=jnp.float32)
                gate_vals = jax.nn.softmax(jnp.take_along_axis(logits, choice_ids, axis=1), axis=-1)
                mixed = moe_routed(normed, choice_ids, gate_vals, w_gate[layer_idx], w_up[layer_idx], w_down[layer_idx], ep_size)
                hidden = (hidden.astype(jnp.float32) + mixed.astype(jnp.float32)).astype(jnp.bfloat16)
                k_list.append(key_new)
                v_list.append(val_new)
            return hidden, jnp.stack(k_list), jnp.stack(v_list)

        def tick_step(tick_idx, loop_state):
            incoming, out_buf, k_buf, v_buf = loop_state
            micro_idx = jnp.clip(tick_idx - stage_idx, 0, micro_count - 1)
            is_valid = (tick_idx >= stage_idx) & (tick_idx - stage_idx < micro_count)
            first_in = lax.dynamic_index_in_dim(hidden_in, micro_idx, 0, keepdims=False)
            stage_in = jnp.where(stage_idx == 0, first_in, incoming)
            result, k_rows, v_rows = run_stage(stage_in, micro_idx)
            old_k = lax.dynamic_index_in_dim(k_buf, micro_idx, 1, keepdims=False)
            k_buf = lax.dynamic_update_index_in_dim(k_buf, jnp.where(is_valid, k_rows, old_k), micro_idx, 1)
            old_v = lax.dynamic_index_in_dim(v_buf, micro_idx, 1, keepdims=False)
            v_buf = lax.dynamic_update_index_in_dim(v_buf, jnp.where(is_valid, v_rows, old_v), micro_idx, 1)
            keep_out = is_valid & (stage_idx == stage_count - 1)
            old_out = lax.dynamic_index_in_dim(out_buf, micro_idx, 0, keepdims=False)
            out_buf = lax.dynamic_update_index_in_dim(out_buf, jnp.where(keep_out, result, old_out), micro_idx, 0)
            incoming = lax.ppermute(result, "pp", shift_perm)
            return incoming, out_buf, k_buf, v_buf

        new_shape = k_cache.shape[:3] + k_cache.shape[4:]
        start_state = (jnp.zeros(hidden_in.shape[1:], jnp.bfloat16), jnp.zeros(hidden_in.shape, jnp.bfloat16), jnp.zeros(new_shape, jnp.bfloat16), jnp.zeros(new_shape, jnp.bfloat16))
        end_state = lax.fori_loop(0, micro_count + stage_count - 1, tick_step, start_state)
        final_out = jnp.where(stage_idx == stage_count - 1, rms_norm(end_state[1], final_gain), jnp.zeros((), jnp.bfloat16))
        return lax.psum(final_out, "pp"), end_state[2], end_state[3]

    return jax.shard_map(device_fn, mesh=mesh, in_specs=in_specs, out_specs=out_specs, check_vma=False)
```

profile of v0, /device:TPU:0, one launch (start us, length us, event | category | flops | bytes accessed | tf_op | source)
XLA Modules:
  0.0 7519.3 jit_solution(2521967264983604498)
XLA Ops:
  19.9 7378.2 %while.22 = (s32[]{:T(128)}, bf16[32,1024]{1,0:T(8,128)(2,1)S(1)}, bf16[64,32,1024]{2,1,0:T(8,128)(2,1)}, bf16[1,64,32,8,64]{4,3,2,1,0:T(8,128)(2,1)}, bf16[1,64...) while((s32[]{:T(128)}, bf16[32,1024]{1,0:T(8,128)(2,1)S(1)}, ...), condition=%wide.region_15.16_spmd, body=%wide.region_0.15_spmd.sunk | while | flops 1015000704 | bytes 55643128 | solution.py:158
  212.7 10.6 ragged-dot-none.2
  326.2 10.6 ragged-dot-none.2
  439.7 10.6 ragged-dot-none.2
  553.2 10.6 ragged-dot-none.2
  666.7 10.6 ragged-dot-none.2
  780.2 10.6 ragged-dot-none.2
  893.7 10.6 ragged-dot-none.2
  1007.2 10.6 ragged-dot-none.2
  1120.7 10.6 ragged-dot-none.2
  1234.2 10.6 ragged-dot-none.2
  1347.7 10.6 ragged-dot-none.2
  1461.2 10.6 ragged-dot-none.2
  1574.7 10.6 ragged-dot-none.2
  1688.2 10.6 ragged-dot-none.2
  1801.7 10.6 ragged-dot-none.2
  1915.2 10.6 ragged-dot-none.2
  2028.7 10.6 ragged-dot-none.2
  2142.1 10.6 ragged-dot-none.2
  2255.6 10.6 ragged-dot-none.2
  2369.1 10.6 ragged-dot-none.2
  2482.6 10.6 ragged-dot-none.2
  2596.1 10.6 ragged-dot-none.2
  2709.6 10.6 ragged-dot-none.2
  2823.1 10.6 ragged-dot-none.2
  2936.6 10.6 ragged-dot-none.2
  3163.6 10.6 ragged-dot-none.2
  3390.6 10.6 ragged-dot-none.2
  3617.6 10.6 ragged-dot-none.2
  3731.1 10.6 ragged-dot-none.2
  4639.1 10.6 ragged-dot-none.2
  4752.6 10.6 ragged-dot-none.2
  4866.1 10.6 ragged-dot-none.2
  4979.6 10.6 ragged-dot-none.2
  5093.1 10.6 ragged-dot-none.2
  5206.6 10.6 ragged-dot-none.2
  5433.5 10.6 ragged-dot-none.2
  5547.0 10.6 ragged-dot-none.2
  5660.5 10.6 ragged-dot-none.2
  5774.0 10.6 ragged-dot-none.2
  5887.5 10.6 ragged-dot-none.2
  6001.0 10.6 ragged-dot-none.2
  6114.5 10.6 ragged-dot-none.2
  6228.0 10.6 ragged-dot-none.2
  6341.5 10.6 ragged-dot-none.2
  6682.0 10.6 ragged-dot-none.2
  7022.5 10.6 ragged-dot-none.2
  7404.3 103.1 %all-reduce.2.cloned.1.call-done = bf16[64,32,1024]{2,1,0:T(8,128)(2,1)} async-done(((bf16[64,32,1024]{2,1,0:T(8,128)(2,1)}), bf16[64,32,1024]{2,1,0:T(8,128)(2,1)}) %all-reduce.2.cloned.1.call-update) | async-done | bytes 4194320 | tf_op jit(solution)/shard_map/psum | solution.py:160
  (7777 shorter events, 6889.4 us)
Async XLA Ops:
  7.2 7500.3 %all-reduce.2.cloned.1.call-start = ((), (), s32[]{:S(2)}) async-start(), calls=%async_computation.3 | async-start | bytes 8388608 | tf_op jit(solution)/shard_map/psum | solution.py:160
  57.4 17.4 all-to-all-start.1
  170.5 17.4 all-to-all-start.1
  397.5 17.4 all-to-all-start.1
  511.0 17.4 all-to-all-start.1
  738.0 17.4 all-to-all-start.1
  851.4 17.4 all-to-all-start.1
  964.9 17.4 all-to-all-start.1
  1078.4 17.4 all-to-all-start.1
  1191.9 17.4 all-to-all-start.1
  1305.4 17.4 all-to-all-start.1
  1418.9 17.4 all-to-all-start.1
  1532.4 17.4 all-to-all-start.1
  1759.4 17.4 all-to-all-start.1
  1872.9 17.4 all-to-all-start.1
  2099.9 17.4 all-to-all-start.1
  2213.4 17.4 all-to-all-start.1
  2440.4 17.4 all-to-all-start.1
  2553.9 17.4 all-to-all-start.1
  2894.3 17.4 all-to-all-start.1
  3007.8 17.4 all-to-all-start.1
  3121.4 17.4 all-to-all-start.1
  3234.9 17.4 all-to-all-start.1
  3461.9 17.4 all-to-all-start.1
  3575.4 17.4 all-to-all-start.1
  3688.9 17.4 all-to-all-start.1
  3915.9 17.4 all-to-all-start.1
  4029.4 17.4 all-to-all-start.1
  4142.9 17.4 all-to-all-start.1
  4256.4 17.4 all-to-all-start.1
  4369.9 17.4 all-to-all-start.1
  4483.4 17.4 all-to-all-start.1
  4596.9 17.4 all-to-all-start.1
  4710.4 17.4 all-to-all-start.1
  4823.8 17.4 all-to-all-start.1
  4937.3 17.4 all-to-all-start.1
  5050.8 17.4 all-to-all-start.1
  5277.8 17.4 all-to-all-start.1
  5391.3 17.4 all-to-all-start.1
  5618.3 17.4 all-to-all-start.1
  5731.8 17.4 all-to-all-start.1
  5958.8 17.4 all-to-all-start.1
  6072.3 17.4 all-to-all-start.1
  6185.8 17.4 all-to-all-start.1
  6299.3 17.4 all-to-all-start.1
  6412.8 17.4 all-to-all-start.1
  6526.3 17.4 all-to-all-start.1
  6639.8 17.4 all-to-all-start.1
  (283 other events, 2643.1 us)
Sparse Core Ops, SparseCore 0:
  7404.5 102.9 all-reduce.1
where the time goes:
time: 7600 us; the launch traced here: 7520 us
  Pallas kernels  2150 us (28%)
  local copies, waits for them, and re-layouts  1690 us (22%)
  other arithmetic  1370 us (18%)
  starting transfers between devices  936 us (12%)
  matrix products  669 us (9%)
  waiting for transfers between devices  663 us (9%)
    another operation x195, Pallas kernels  2050 us
    all_to_all x65, waiting for transfers between devices, moe_routed(): back_rows = lax.all_to_all(weighted, 'ep', 0, 0, tiled=True)  453 us
    ppermute x65, starting transfers between devices, tick_step(): incoming = lax.ppermute(result, 'pp', shift_perm)  276 us
    all_to_all x65, starting transfers between devices, moe_routed(): recv_rows = lax.all_to_all(send_rows, 'ep', 0, 0, tiled=True)  226 us
    all_to_all x65, starting transfers between devices, moe_routed(): back_rows = lax.all_to_all(weighted, 'ep', 0, 0, tiled=True)  225 us
    all_to_all x65, starting transfers between devices, moe_routed(): recv_meta = lax.all_to_all(send_meta, 'ep', 0, 0, tiled=True)  209 us
    sort x65, other arithmetic, expert_rows(): sort_order = jnp.argsort(labels, stable=True)  206 us
    sort x65, other arithmetic, expert_rows(): return weighted[jnp.argsort(sort_order)]  206 us

commit v1 on v0

v1 whole, which is shorter than its diff:
```python
import functools

import jax
import jax.numpy as jnp
from jax import lax
from jax.experimental import pallas as pl
from jax.experimental.pallas import tpu as pltpu
from jax.sharding import PartitionSpec as P

THETA = 1000000.0
EPS = 1e-05
F32 = jnp.float32
BF16 = jnp.bfloat16
TILE = 128
GROUP = 16


def rms(vals, gain_row):
    inv = lax.rsqrt(jnp.mean(vals * vals, axis=-1, keepdims=True) + EPS)
    return (vals * inv * gain_row).astype(BF16)


def dot_nt(lhs, rhs):
    return lax.dot_general(lhs, rhs, (((1,), (1,)), ((), ())), preferred_element_type=F32)


def dot_tn(lhs, rhs):
    return lax.dot_general(lhs, rhs, (((0,), (0,)), ((), ())), preferred_element_type=F32)


def dot(lhs, rhs):
    return jnp.dot(lhs, rhs, preferred_element_type=F32)


def rope_table(pos, table_ref):
    picked = jnp.zeros(pos.shape, F32)
    for t in range(table_ref.shape[0]):
        picked = jnp.where(pos == t + 1, table_ref[t:t + 1, :], picked)
    return picked


def rope(vals, cos_t, sin_t):
    lane = lax.broadcasted_iota(jnp.int32, (1, 128), 1)
    first = (lane % 64) < 32
    parts = []
    for j in range(vals.shape[1] // 128):
        block = vals[:, j * 128:(j + 1) * 128]
        swapped = jnp.where(first, pltpu.roll(block, 96, 1), pltpu.roll(block, 32, 1))
        parts.append(block * cos_t + swapped * sin_t)
    return jnp.concatenate(parts, axis=1)


def attn_project(hidden, pos, w_q, w_k, w_v, gain, cos_ref, sin_ref, q3, k3, v3):
    tokens = hidden.shape[0]
    normed = rms(hidden.astype(F32), gain[...].astype(F32))
    cos_t = rope_table(pos, cos_ref)
    sin_t = rope_table(pos, sin_ref)
    q = rope(dot(normed, w_q[...]).astype(BF16).astype(F32), cos_t, sin_t)
    q3[...] = q.astype(BF16).astype(F32).reshape(tokens, -1, 128)
    k = rope(dot(normed, w_k[...]).astype(BF16).astype(F32), cos_t, sin_t)
    k3[...] = k.astype(BF16).astype(F32).reshape(tokens, -1, 128)
    v3[...] = dot(normed, w_v[...]).astype(BF16).astype(F32).reshape(tokens, -1, 128)


def attn_group(idx, q3, k3, v3, o3, pos_ref, k_rows, v_rows):
    base = pl.multiple_of(idx * GROUP, GROUP)
    span = pl.ds(base, GROUP)
    q = q3[span]
    lane3 = lax.broadcasted_iota(jnp.int32, (1, 1, 128), 2)
    prod = q * k3[span]
    self_a = jnp.sum(jnp.where(lane3 < 64, prod, 0.0), axis=-1, keepdims=True)
    self_b = jnp.sum(jnp.where(lane3 < 64, 0.0, prod), axis=-1, keepdims=True)
    self_s = jnp.concatenate([self_a, self_b], axis=1) * 0.125
    q_rows = jnp.concatenate([q, pltpu.roll(q, 64, 2)], axis=1).astype(BF16)[:, :, :64].reshape(GROUP * 16, 64)
    row0 = idx * (GROUP * 128)
    blocks = []
    for p in range(GROUP // 2):
        keys = k_rows[pl.ds(pl.multiple_of(row0 + p * 256, 256), 256), :]
        both = dot_nt(q_rows[p * 32:(p + 1) * 32], keys)
        blocks.append(both[:16, :128].reshape(1, 16, 128))
        blocks.append(both[16:, 128:].reshape(1, 16, 128))
    scores = jnp.concatenate(blocks, axis=0)
    row_i = lax.broadcasted_iota(jnp.int32, (16, 128), 0)
    lane_i = lax.broadcasted_iota(jnp.int32, (16, 128), 1)
    step = jnp.where((row_i % 8) == (lane_i % 8), lane_i // 8, 1000)
    pos = pos_ref[span, :].reshape(GROUP, 1, 128)
    scores = jnp.where(step.reshape(1, 16, 128) < pos, scores * 0.125, -jnp.inf)
    top = jnp.maximum(jnp.max(scores, axis=-1, keepdims=True), self_s)
    weights = jnp.exp(scores - top)
    self_w = jnp.exp(self_s - top)
    inv = 1.0 / (jnp.sum(weights, axis=-1, keepdims=True) + self_w)
    weights = (weights * inv).astype(BF16)
    self_w = (self_w * inv).astype(BF16).astype(F32)
    zeros = jnp.zeros((16, 128), BF16)
    outs = []
    for p in range(GROUP // 2):
        vals = v_rows[pl.ds(pl.multiple_of(row0 + p * 256, 256), 256), :]
        upper = jnp.concatenate([weights[2 * p], zeros], axis=1)
        lower = jnp.concatenate([zeros, weights[2 * p + 1]], axis=1)
        outs.append(dot(jnp.concatenate([upper, lower], axis=0), vals).reshape(2, 16, 64))
    out = jnp.concatenate(outs, axis=0)
    v_new = v3[span][:, :, :64]
    out_a = out[:, :8] + self_w[:, :8] * v_new
    out_b = out[:, 8:] + self_w[:, 8:] * v_new
    o3[span] = jnp.concatenate([out_a, out_b], axis=-1)


def attn_finish(hidden, o3, w_o, gain):
    tokens = hidden.shape[0]
    out = o3[...].reshape(tokens, 1024).astype(BF16)
    mid = (hidden.astype(F32) + dot(out, w_o[...])).astype(BF16)
    return mid, rms(mid.astype(F32), gain[...].astype(F32))


def attn_kernel(h_ref, pos_ref, k_rows, v_rows, w_q, w_k, w_v, w_o, a_gain, m_gain, cos_ref, sin_ref, mid_ref, n_ref, kn_ref, vn_ref, q3, k3, v3, o3):
    hidden = h_ref[...]
    attn_project(hidden, pos_ref[...], w_q, w_k, w_v, a_gain, cos_ref, sin_ref, q3, k3, v3)
    kn_ref[...] = k3[...][:, :, :64].astype(BF16)
    vn_ref[...] = v3[...][:, :, :64].astype(BF16)

    def body(idx, carry):
        attn_group(idx, q3, k3, v3, o3, pos_ref, k_rows, v_rows)
        return carry

    lax.fori_loop(0, hidden.shape[0] // GROUP, body, 0)
    mid, normed = attn_finish(hidden, o3, w_o, m_gain)
    mid_ref[...] = mid
    n_ref[...] = normed


def moe_route(ids, first, normed, w_r, tri, rank_ref, gate_ref):
    tokens = ids.shape[1]
    expert_i = lax.broadcasted_iota(jnp.int32, (32, tokens), 0)
    chosen = jnp.zeros((32, tokens), F32)
    for s in range(ids.shape[0]):
        chosen = jnp.where(ids[s:s + 1, :] == expert_i, 1.0, chosen)
    rank = dot(chosen.astype(BF16), tri[...])
    rank_ref[...] = jnp.where(chosen > 0.0, rank, -1.0)
    logits = dot_nt(w_r[...], normed)
    top = jnp.max(jnp.where(chosen > 0.0, logits, -jnp.inf), axis=0, keepdims=True)
    gates = jnp.where(chosen > 0.0, jnp.exp(logits - top), 0.0)
    gate_ref[...] = gates / jnp.sum(gates, axis=0, keepdims=True)


def moe_tile(expert, sub, first, n_ref, rank_ref, gate_ref, w_g, w_u, w_d, acc):
    tokens = n_ref.shape[0]
    ranks = rank_ref[pl.ds(first + expert, 1), :]
    wanted = (lax.broadcasted_iota(jnp.int32, (TILE, 1), 0) + sub * TILE).astype(F32)
    picked = jnp.where(ranks == wanted, 1.0, 0.0)
    gate = jnp.sum(picked * gate_ref[pl.ds(first + expert, 1), :], axis=-1, keepdims=True)
    onehot = picked.astype(BF16)
    rows = dot(onehot, n_ref[...]).astype(BF16)
    up = jax.nn.silu(dot(rows, w_g[expert])) * dot(rows, w_u[expert])
    term = (gate * dot(up.astype(BF16), w_d[expert])).astype(BF16)
    acc[...] += dot_tn(onehot, term)


def moe_kernel(te_ref, tk_ref, first_ref, n_ref, ids_ref, w_r, w_g, w_u, w_d, tri, out_ref, rank_ref, gate_ref):
    first = first_ref[0]
    moe_route(ids_ref[...], first, n_ref[...], w_r, tri, rank_ref, gate_ref)
    out_ref[...] = jnp.zeros_like(out_ref)

    def body(idx, carry):
        moe_tile(te_ref[idx], tk_ref[idx], first, n_ref, rank_ref, gate_ref, w_g, w_u, w_d, out_ref)
        return carry

    lax.fori_loop(0, te_ref.shape[0], body, 0)


def vmem_spec():
    return pl.BlockSpec(memory_space=pltpu.VMEM)


def smem_spec():
    return pl.BlockSpec(memory_space=pltpu.SMEM)


def attn_call(hidden, pos, k_rows, v_rows, consts):
    tokens = hidden.shape[0]
    big = pltpu.VMEM((tokens, 8, 128), F32)
    return pl.pallas_call(
        attn_kernel,
        out_shape=(
            jax.ShapeDtypeStruct((tokens, 1024), BF16),
            jax.ShapeDtypeStruct((tokens, 1024), BF16),
            jax.ShapeDtypeStruct((tokens, 8, 64), BF16),
            jax.ShapeDtypeStruct((tokens, 8, 64), BF16),
        ),
        in_specs=[vmem_spec()] * 12,
        out_specs=(vmem_spec(),) * 4,
        scratch_shapes=[big, big, big, big],
        name="attn_chunk",
        cost_estimate=pl.CostEstimate(flops=4 * 10**9, bytes_accessed=20 * 10**6, transcendentals=0),
    )(hidden, pos, k_rows, v_rows, *consts)


def moe_call(normed, ids, te, tk, first, w_r, w_g, w_u, w_d, tri):
    tokens = normed.shape[0]
    return pl.pallas_call(
        moe_kernel,
        out_shape=jax.ShapeDtypeStruct((tokens, 1024), F32),
        in_specs=[smem_spec()] * 3 + [vmem_spec()] * 7,
        out_specs=vmem_spec(),
        scratch_shapes=[pltpu.VMEM((32, tokens), F32), pltpu.VMEM((32, tokens), F32)],
        name="moe_chunk",
        cost_estimate=pl.CostEstimate(flops=10**10, bytes_accessed=30 * 10**6, transcendentals=0),
    )(te, tk, first, normed, ids, w_r, w_g, w_u, w_d, tri)


def dup_heads(w):
    rows = w.shape[0]
    heads = w.reshape(rows, -1, 1, 64)
    return jnp.broadcast_to(heads, (rows, heads.shape[1], 2, 64)).reshape(rows, -1)


def tile_tables(ids, first, tile_count):
    local = first + jnp.arange(8, dtype=jnp.int32)
    counts = jnp.sum((ids[:, None] == local[None, :, None, None]).astype(jnp.int32), axis=(2, 3))
    tiles = (counts + TILE - 1) // TILE
    ends = jnp.cumsum(tiles, axis=1)
    idx = jnp.arange(tile_count, dtype=jnp.int32)
    expert = jnp.sum((idx[None, :, None] >= ends[:, None, :]).astype(jnp.int32), axis=-1)
    safe = jnp.minimum(expert, 7)
    starts = ends - tiles
    start = jnp.sum(jnp.where(safe[:, :, None] == jnp.arange(8)[None, None, :], starts[:, None, :], 0), axis=-1)
    sub = jnp.where(expert < 8, idx[None, :] - start, 1000)
    return safe, sub.astype(jnp.int32)


def solution(mesh):
    ep_size = mesh.shape["ep"]
    stage_count = mesh.shape["pp"]
    rows_spec = ("dp", "ep")
    three_dim = P("pp", None, None)
    two_dim = P("pp", None)
    expert_spec = P("pp", "ep", None, None)
    cache_spec = P("pp", None, rows_spec, None, None, None)
    new_spec = P("pp", None, rows_spec, None, None)
    in_specs = (P(None, rows_spec, None), P(None, rows_spec), cache_spec, cache_spec, P("pp", None, rows_spec, None), three_dim, three_dim, three_dim, three_dim, two_dim, two_dim, three_dim, expert_spec, expert_spec, expert_spec, P(None))
    out_specs = (P(None, rows_spec, None), new_spec, new_spec)
    shift_perm = [(s, s + 1) for s in range(stage_count - 1)]
    per_chunk = 4

    def device_fn(hidden_in, seq_pos, k_cache, v_cache, expert_ids, w_query, w_key, w_value, w_out, attn_gain, mlp_gain, w_router, w_gate, w_up, w_down, final_gain):
        stage = lax.axis_index("pp")
        ep_idx = lax.axis_index("ep")
        micro, rows = seq_pos.shape
        chunks = micro // per_chunk
        tokens = per_chunk * rows
        gathered = ep_size * tokens
        tile_count = gathered * 2 // TILE + 7
        hid = hidden_in.reshape(chunks, tokens, 1024)
        pos = jnp.broadcast_to(seq_pos.reshape(micro * rows, 1), (micro * rows, 128)).reshape(chunks, tokens, 128)
        k_rows = k_cache.reshape(chunks, tokens * 128, 64)
        v_rows = v_cache.reshape(chunks, tokens * 128, 64)
        inv_freq = THETA ** (-jnp.arange(32, dtype=F32) / 32)
        angles = jnp.arange(1, 17, dtype=F32)[:, None] * inv_freq
        cos_t = jnp.tile(jnp.cos(angles), (1, 4))
        sin_t = jnp.tile(jnp.concatenate([-jnp.sin(angles), jnp.sin(angles)], axis=1), (1, 2))
        consts = (w_query[0], dup_heads(w_key[0]), dup_heads(w_value[0]), w_out[0], attn_gain, mlp_gain, cos_t, sin_t)
        first = (ep_idx * 8).astype(jnp.int32).reshape(1)
        ids = lax.all_gather(expert_ids[0].reshape(chunks, tokens, 8), "ep", axis=1, tiled=True)
        ids = jnp.swapaxes(ids, 1, 2)
        te, tk = tile_tables(ids, first[0], tile_count)
        ti = jnp.arange(gathered)
        tri = (ti[:, None] < ti[None, :]).astype(BF16)
        router_t = w_router[0].T

        def tick(t, state):
            incoming, out_buf, k_buf, v_buf = state
            c = jnp.clip(t - stage, 0, chunks - 1)
            at = lambda arr: lax.dynamic_index_in_dim(arr, c, 0, keepdims=False)
            stage_in = jnp.where(stage == 0, at(hid), incoming)
            mid, normed, k_new, v_new = attn_call(stage_in, at(pos), at(k_rows), at(v_rows), consts)
            n_all = lax.all_gather(normed, "ep", axis=0, tiled=True)
            part = moe_call(n_all, at(ids), at(te), at(tk), first, router_t, w_gate[0], w_up[0], w_down[0], tri)
            mixed = lax.psum_scatter(part, "ep", scatter_dimension=0, tiled=True).astype(BF16)
            result = (mid.astype(F32) + mixed.astype(F32)).astype(BF16)
            k_buf = lax.dynamic_update_index_in_dim(k_buf, k_new, c, 0)
            v_buf = lax.dynamic_update_index_in_dim(v_buf, v_new, c, 0)
            out_buf = lax.dynamic_update_index_in_dim(out_buf, result, c, 0)
            return lax.ppermute(result, "pp", shift_perm), out_buf, k_buf, v_buf

        state = (jnp.zeros((tokens, 1024), BF16), jnp.zeros(hid.shape, BF16), jnp.zeros((chunks, tokens, 8, 64), BF16), jnp.zeros((chunks, tokens, 8, 64), BF16))
        _, out_buf, k_buf, v_buf = lax.fori_loop(0, chunks + stage_count - 1, tick, state)
        x = out_buf.reshape(hidden_in.shape).astype(F32)
        final = rms(x, final_gain.astype(F32))
        final = jnp.where(stage == stage_count - 1, final, jnp.zeros((), BF16))
        shape = (1,) + seq_pos.shape + (8, 64)
        return lax.psum(final, "pp"), k_buf.reshape(shape), v_buf.reshape(shape)

    return jax.shard_map(device_fn, mesh=mesh, in_specs=in_specs, out_specs=out_specs, check_vma=False)
```

time: 7600 us -> 2070 us (0.27)
  Pallas kernels: 2150 us -> 740 us
  local copies, waits for them, and re-layouts: 1690 us -> 343 us
  other arithmetic: 1370 us -> 84.2 us
  starting transfers between devices: 936 us -> 58 us
  matrix products: 669 us -> 0 us
  waiting for transfers between devices: 663 us -> 810 us
    another operation x195 -> x0, Pallas kernels: 2050 us -> none
    gather x715 -> x0, local copies, waits for them, and re-layouts: 1050 us -> none  [the longest x195 139 us: run_stage(): jnp.take_along_axis(logits, choice_ids, axis=1)]
    pallas_call x0 -> x34, Pallas kernels: none -> 740 us  [the longest x17 485 us: moe_call(): pl.pallas_call(moe_kernel, out_shape=jax.ShapeDtypeStruct((tokens, 1024),...]
    dot_general x520 -> x0, matrix products: 669 us -> none  [the longest x65 139 us: attend(): jnp.einsum('bkgt,btkh->bkgh', cache_w, v_rows, preferred_element_type=jnp...]
    all_to_all x195 -> x0, starting transfers between devices: 660 us -> none  [the longest x65 226 us: moe_routed(): recv_rows = lax.all_to_all(send_rows, 'ep', 0, 0, tiled=True)]
    all_to_all x195 -> x0, waiting for transfers between devices: 542 us -> none  [the longest x65 453 us: moe_routed(): back_rows = lax.all_to_all(weighted, 'ep', 0, 0, tiled=True)]
    reduce_scatter x0 -> x17, waiting for transfers between devices: none -> 437 us  [tick(): lax.psum_scatter(part, 'ep', scatter_dimension=0, tiled=True).astype(BF16)]
    sort x130 -> x0, other arithmetic: 413 us -> none  [the longest x65 206 us: expert_rows(): sort_order = jnp.argsort(labels, stable=True)]
where the time goes in v1:
time: 2070 us; the launch traced here: 2060 us
  waiting for transfers between devices  810 us (39%)
  Pallas kernels  740 us (36%)
  local copies, waits for them, and re-layouts  343 us (17%)
  other arithmetic  84.2 us (4%)
  starting transfers between devices  58 us (3%)
    pallas_call x17, Pallas kernels, moe_call(): pl.pallas_call(moe_kernel, out_shape=jax.ShapeDtypeStruct((tokens, 1024),...  485 us
    reduce_scatter x17, waiting for transfers between devices, tick(): lax.psum_scatter(part, 'ep', scatter_dimension=0, tiled=True).astype(BF16)  437 us
    pallas_call x17, Pallas kernels, attn_call(): pl.pallas_call(attn_kernel, out_shape=(jax.ShapeDtypeStruct((tokens, 1024...  255 us
    all_gather x17, waiting for transfers between devices, tick(): n_all = lax.all_gather(normed, 'ep', axis=0, tiled=True)  205 us
    squeeze x68, local copies, waits for them, and re-layouts, tick(): at = lambda arr: lax.dynamic_index_in_dim(arr, c, 0, keepdims=False)  157 us
    psum x1, waiting for transfers between devices, device_fn(): return (lax.psum(final, 'pp'), k_buf.reshape(shape), v_buf.reshape(shape))  103 us
    reshape x34, local copies, waits for them, and re-layouts, dup_heads(): jnp.broadcast_to(heads, (rows, heads.shape[1], 2, 64)).reshape(rows, -1)  87.8 us
    ppermute x17, waiting for transfers between devices, tick(): return (lax.ppermute(result, 'pp', shift_perm), out_buf, k_buf, v_buf)  64.7 us
  transfers between devices with their start and end apart: 52, of which 52 were waited for; matrix products, arithmetic and copies ran while one was open for 3% of the time, Pallas kernels for 0%

profile of v1, /device:TPU:0, one launch (start us, length us, event | category | flops | bytes accessed | tf_op | source)
XLA Modules:
  0.0 2062.4 jit_solution(16668861709169130439)
XLA Ops:
  37.2 1902.1 %while.21 = (s32[]{:T(128)}, bf16[128,1024]{1,0:T(8,128)(2,1)S(1)}, bf16[16,128,1024]{2,1,0:T(8,128)(2,1)}, bf16[16,128,8,64]{3,2,1,0:T(8,128)(2,1)}, bf16[16,12...) while((s32[]{:T(128)}, bf16[128,1024]{1,0:T(8,128)(2,1)S(1)}, ...), condition=%wide.region_6.7_spmd.clone, body=%wide.region_4.6_spmd.clone.sunk | while | flops 14001310720 | bytes 100027304 | solution.py:285
  54.6 15.0 attn_chunk.6
  83.6 28.5 %moe_chunk.6 = f32[512,1024]{1,0:T(8,128)} custom-call(s32[15]{0:T(128)} %get-tuple-element.885.te_ref, s32[15]{0:T(128)} %get-tuple-element.886.tk_ref, s32[1]{0:T(128)} %get-tuple-element.976.first_ref, bf16[512,1024]{1,0:T(8,128)(2,1)} %all-gather.2.cloned.1.call-done.n_ref, s32[8,512]{1,0:T(8,128)} %dynamic-slice_bitcast_fusion.9.ids_ref, ...), custom_call_target="tpu_custom_call" | custom-call | flops 10000000000 | bytes 30000000 | tf_op jit(solution)/shard_map/while/body/eval_jaxpr/moe_chunk/pallas_call | solution.py:199
  112.1 25.7 %reduce-scatter.2.cloned.1.call-done = f32[128,1024]{1,0:T(8,128)} async-done(((f32[512,1024]{1,0:T(8,128)}), f32[128,1024]{1,0:T(8,128)}) %reduce-scatter.2.cloned.1.call-update) | async-done | bytes 524304 | tf_op jit(solution)/shard_map/while/body/eval_jaxpr/reduce_scatter | solution.py:277
  195.6 28.5 %moe_chunk.6 = f32[512,1024]{1,0:T(8,128)} custom-call(s32[15]{0:T(128)} %get-tuple-element.885.te_ref, s32[15]{0:T(128)} %get-tuple-element.886.tk_ref, s32[1]{0:T(128)} %get-tuple-element.976.first_ref, bf16[512,1024]{1,0:T(8,128)(2,1)} %all-gather.2.cloned.1.call-done.n_ref, s32[8,512]{1,0:T(8,128)} %dynamic-slice_bitcast_fusion.9.ids_ref, ...), custom_call_target="tpu_custom_call" | custom-call | flops 10000000000 | bytes 30000000 | tf_op jit(solution)/shard_map/while/body/eval_jaxpr/moe_chunk/pallas_call | solution.py:199
  224.1 25.7 %reduce-scatter.2.cloned.1.call-done = f32[128,1024]{1,0:T(8,128)} async-done(((f32[512,1024]{1,0:T(8,128)}), f32[128,1024]{1,0:T(8,128)}) %reduce-scatter.2.cloned.1.call-update) | async-done | bytes 524304 | tf_op jit(solution)/shard_map/while/body/eval_jaxpr/reduce_scatter | solution.py:277
  277.5 15.0 attn_chunk.6
  307.5 28.5 %moe_chunk.6 = f32[512,1024]{1,0:T(8,128)} custom-call(s32[15]{0:T(128)} %get-tuple-element.885.te_ref, s32[15]{0:T(128)} %get-tuple-element.886.tk_ref, s32[1]{0:T(128)} %get-tuple-element.976.first_ref, bf16[512,1024]{1,0:T(8,128)(2,1)} %all-gather.2.cloned.1.call-done.n_ref, s32[8,512]{1,0:T(8,128)} %dynamic-slice_bitcast_fusion.9.ids_ref, ...), custom_call_target="tpu_custom_call" | custom-call | flops 10000000000 | bytes 30000000 | tf_op jit(solution)/shard_map/while/body/eval_jaxpr/moe_chunk/pallas_call | solution.py:199
  336.0 25.7 %reduce-scatter.2.cloned.1.call-done = f32[128,1024]{1,0:T(8,128)} async-done(((f32[512,1024]{1,0:T(8,128)}), f32[128,1024]{1,0:T(8,128)}) %reduce-scatter.2.cloned.1.call-update) | async-done | bytes 524304 | tf_op jit(solution)/shard_map/while/body/eval_jaxpr/reduce_scatter | solution.py:277
  389.5 15.0 attn_chunk.6
  419.4 28.5 %moe_chunk.6 = f32[512,1024]{1,0:T(8,128)} custom-call(s32[15]{0:T(128)} %get-tuple-element.885.te_ref, s32[15]{0:T(128)} %get-tuple-element.886.tk_ref, s32[1]{0:T(128)} %get-tuple-element.976.first_ref, bf16[512,1024]{1,0:T(8,128)(2,1)} %all-gather.2.cloned.1.call-done.n_ref, s32[8,512]{1,0:T(8,128)} %dynamic-slice_bitcast_fusion.9.ids_ref, ...), custom_call_target="tpu_custom_call" | custom-call | flops 10000000000 | bytes 30000000 | tf_op jit(solution)/shard_map/while/body/eval_jaxpr/moe_chunk/pallas_call | solution.py:199
  448.0 25.7 %reduce-scatter.2.cloned.1.call-done = f32[128,1024]{1,0:T(8,128)} async-done(((f32[512,1024]{1,0:T(8,128)}), f32[128,1024]{1,0:T(8,128)}) %reduce-scatter.2.cloned.1.call-update) | async-done | bytes 524304 | tf_op jit(solution)/shard_map/while/body/eval_jaxpr/reduce_scatter | solution.py:277
  501.4 15.0 attn_chunk.6
  531.4 28.5 %moe_chunk.6 = f32[512,1024]{1,0:T(8,128)} custom-call(s32[15]{0:T(128)} %get-tuple-element.885.te_ref, s32[15]{0:T(128)} %get-tuple-element.886.tk_ref, s32[1]{0:T(128)} %get-tuple-element.976.first_ref, bf16[512,1024]{1,0:T(8,128)(2,1)} %all-gather.2.cloned.1.call-done.n_ref, s32[8,512]{1,0:T(8,128)} %dynamic-slice_bitcast_fusion.9.ids_ref, ...), custom_call_target="tpu_custom_call" | custom-call | flops 10000000000 | bytes 30000000 | tf_op jit(solution)/shard_map/while/body/eval_jaxpr/moe_chunk/pallas_call | solution.py:199
  559.9 25.7 %reduce-scatter.2.cloned.1.call-done = f32[128,1024]{1,0:T(8,128)} async-done(((f32[512,1024]{1,0:T(8,128)}), f32[128,1024]{1,0:T(8,128)}) %reduce-scatter.2.cloned.1.call-update) | async-done | bytes 524304 | tf_op jit(solution)/shard_map/while/body/eval_jaxpr/reduce_scatter | solution.py:277
  613.3 15.0 attn_chunk.6
  643.3 28.5 %moe_chunk.6 = f32[512,1024]{1,0:T(8,128)} custom-call(s32[15]{0:T(128)} %get-tuple-element.885.te_ref, s32[15]{0:T(128)} %get-tuple-element.886.tk_ref, s32[1]{0:T(128)} %get-tuple-element.976.first_ref, bf16[512,1024]{1,0:T(8,128)(2,1)} %all-gather.2.cloned.1.call-done.n_ref, s32[8,512]{1,0:T(8,128)} %dynamic-slice_bitcast_fusion.9.ids_ref, ...), custom_call_target="tpu_custom_call" | custom-call | flops 10000000000 | bytes 30000000 | tf_op jit(solution)/shard_map/while/body/eval_jaxpr/moe_chunk/pallas_call | solution.py:199
  671.8 25.7 %reduce-scatter.2.cloned.1.call-done = f32[128,1024]{1,0:T(8,128)} async-done(((f32[512,1024]{1,0:T(8,128)}), f32[128,1024]{1,0:T(8,128)}) %reduce-scatter.2.cloned.1.call-update) | async-done | bytes 524304 | tf_op jit(solution)/shard_map/while/body/eval_jaxpr/reduce_scatter | solution.py:277
  725.3 15.0 attn_chunk.6
  755.3 28.5 %moe_chunk.6 = f32[512,1024]{1,0:T(8,128)} custom-call(s32[15]{0:T(128)} %get-tuple-element.885.te_ref, s32[15]{0:T(128)} %get-tuple-element.886.tk_ref, s32[1]{0:T(128)} %get-tuple-element.976.first_ref, bf16[512,1024]{1,0:T(8,128)(2,1)} %all-gather.2.cloned.1.call-done.n_ref, s32[8,512]{1,0:T(8,128)} %dynamic-slice_bitcast_fusion.9.ids_ref, ...), custom_call_target="tpu_custom_call" | custom-call | flops 10000000000 | bytes 30000000 | tf_op jit(solution)/shard_map/while/body/eval_jaxpr/moe_chunk/pallas_call | solution.py:199
  783.8 25.7 %reduce-scatter.2.cloned.1.call-done = f32[128,1024]{1,0:T(8,128)} async-done(((f32[512,1024]{1,0:T(8,128)}), f32[128,1024]{1,0:T(8,128)}) %reduce-scatter.2.cloned.1.call-update) | async-done | bytes 524304 | tf_op jit(solution)/shard_map/while/body/eval_jaxpr/reduce_scatter | solution.py:277
  837.2 15.0 attn_chunk.6
  867.2 28.5 %moe_chunk.6 = f32[512,1024]{1,0:T(8,128)} custom-call(s32[15]{0:T(128)} %get-tuple-element.885.te_ref, s32[15]{0:T(128)} %get-tuple-element.886.tk_ref, s32[1]{0:T(128)} %get-tuple-element.976.first_ref, bf16[512,1024]{1,0:T(8,128)(2,1)} %all-gather.2.cloned.1.call-done.n_ref, s32[8,512]{1,0:T(8,128)} %dynamic-slice_bitcast_fusion.9.ids_ref, ...), custom_call_target="tpu_custom_call" | custom-call | flops 10000000000 | bytes 30000000 | tf_op jit(solution)/shard_map/while/body/eval_jaxpr/moe_chunk/pallas_call | solution.py:199
  895.7 25.7 %reduce-scatter.2.cloned.1.call-done = f32[128,1024]{1,0:T(8,128)} async-done(((f32[512,1024]{1,0:T(8,128)}), f32[128,1024]{1,0:T(8,128)}) %reduce-scatter.2.cloned.1.call-update) | async-done | bytes 524304 | tf_op jit(solution)/shard_map/while/body/eval_jaxpr/reduce_scatter | solution.py:277
  949.2 15.0 attn_chunk.6
  979.1 28.5 %moe_chunk.6 = f32[512,1024]{1,0:T(8,128)} custom-call(s32[15]{0:T(128)} %get-tuple-element.885.te_ref, s32[15]{0:T(128)} %get-tuple-element.886.tk_ref, s32[1]{0:T(128)} %get-tuple-element.976.first_ref, bf16[512,1024]{1,0:T(8,128)(2,1)} %all-gather.2.cloned.1.call-done.n_ref, s32[8,512]{1,0:T(8,128)} %dynamic-slice_bitcast_fusion.9.ids_ref, ...), custom_call_target="tpu_custom_call" | custom-call | flops 10000000000 | bytes 30000000 | tf_op jit(solution)/shard_map/while/body/eval_jaxpr/moe_chunk/pallas_call | solution.py:199
  1007.7 25.7 %reduce-scatter.2.cloned.1.call-done = f32[128,1024]{1,0:T(8,128)} async-done(((f32[512,1024]{1,0:T(8,128)}), f32[128,1024]{1,0:T(8,128)}) %reduce-scatter.2.cloned.1.call-update) | async-done | bytes 524304 | tf_op jit(solution)/shard_map/while/body/eval_jaxpr/reduce_scatter | solution.py:277
  1061.1 15.0 attn_chunk.6
  1091.1 28.5 %moe_chunk.6 = f32[512,1024]{1,0:T(8,128)} custom-call(s32[15]{0:T(128)} %get-tuple-element.885.te_ref, s32[15]{0:T(128)} %get-tuple-element.886.tk_ref, s32[1]{0:T(128)} %get-tuple-element.976.first_ref, bf16[512,1024]{1,0:T(8,128)(2,1)} %all-gather.2.cloned.1.call-done.n_ref, s32[8,512]{1,0:T(8,128)} %dynamic-slice_bitcast_fusion.9.ids_ref, ...), custom_call_target="tpu_custom_call" | custom-call | flops 10000000000 | bytes 30000000 | tf_op jit(solution)/shard_map/while/body/eval_jaxpr/moe_chunk/pallas_call | solution.py:199
  1119.6 25.7 %reduce-scatter.2.cloned.1.call-done = f32[128,1024]{1,0:T(8,128)} async-done(((f32[512,1024]{1,0:T(8,128)}), f32[128,1024]{1,0:T(8,128)}) %reduce-scatter.2.cloned.1.call-update) | async-done | bytes 524304 | tf_op jit(solution)/shard_map/while/body/eval_jaxpr/reduce_scatter | solution.py:277
  1173.1 15.0 attn_chunk.6
  1203.0 28.5 %moe_chunk.6 = f32[512,1024]{1,0:T(8,128)} custom-call(s32[15]{0:T(128)} %get-tuple-element.885.te_ref, s32[15]{0:T(128)} %get-tuple-element.886.tk_ref, s32[1]{0:T(128)} %get-tuple-element.976.first_ref, bf16[512,1024]{1,0:T(8,128)(2,1)} %all-gather.2.cloned.1.call-done.n_ref, s32[8,512]{1,0:T(8,128)} %dynamic-slice_bitcast_fusion.9.ids_ref, ...), custom_call_target="tpu_custom_call" | custom-call | flops 10000000000 | bytes 30000000 | tf_op jit(solution)/shard_map/while/body/eval_jaxpr/moe_chunk/pallas_call | solution.py:199
  1231.5 25.7 %reduce-scatter.2.cloned.1.call-done = f32[128,1024]{1,0:T(8,128)} async-done(((f32[512,1024]{1,0:T(8,128)}), f32[128,1024]{1,0:T(8,128)}) %reduce-scatter.2.cloned.1.call-update) | async-done | bytes 524304 | tf_op jit(solution)/shard_map/while/body/eval_jaxpr/reduce_scatter | solution.py:277
  1285.0 15.0 attn_chunk.6
  1315.0 28.5 %moe_chunk.6 = f32[512,1024]{1,0:T(8,128)} custom-call(s32[15]{0:T(128)} %get-tuple-element.885.te_ref, s32[15]{0:T(128)} %get-tuple-element.886.tk_ref, s32[1]{0:T(128)} %get-tuple-element.976.first_ref, bf16[512,1024]{1,0:T(8,128)(2,1)} %all-gather.2.cloned.1.call-done.n_ref, s32[8,512]{1,0:T(8,128)} %dynamic-slice_bitcast_fusion.9.ids_ref, ...), custom_call_target="tpu_custom_call" | custom-call | flops 10000000000 | bytes 30000000 | tf_op jit(solution)/shard_map/while/body/eval_jaxpr/moe_chunk/pallas_call | solution.py:199
  1343.5 25.7 %reduce-scatter.2.cloned.1.call-done = f32[128,1024]{1,0:T(8,128)} async-done(((f32[512,1024]{1,0:T(8,128)}), f32[128,1024]{1,0:T(8,128)}) %reduce-scatter.2.cloned.1.call-update) | async-done | bytes 524304 | tf_op jit(solution)/shard_map/while/body/eval_jaxpr/reduce_scatter | solution.py:277
  1396.9 15.0 attn_chunk.6
  1426.9 28.5 %moe_chunk.6 = f32[512,1024]{1,0:T(8,128)} custom-call(s32[15]{0:T(128)} %get-tuple-element.885.te_ref, s32[15]{0:T(128)} %get-tuple-element.886.tk_ref, s32[1]{0:T(128)} %get-tuple-element.976.first_ref, bf16[512,1024]{1,0:T(8,128)(2,1)} %all-gather.2.cloned.1.call-done.n_ref, s32[8,512]{1,0:T(8,128)} %dynamic-slice_bitcast_fusion.9.ids_ref, ...), custom_call_target="tpu_custom_call" | custom-call | flops 10000000000 | bytes 30000000 | tf_op jit(solution)/shard_map/while/body/eval_jaxpr/moe_chunk/pallas_call | solution.py:199
  1455.4 25.7 %reduce-scatter.2.cloned.1.call-done = f32[128,1024]{1,0:T(8,128)} async-done(((f32[512,1024]{1,0:T(8,128)}), f32[128,1024]{1,0:T(8,128)}) %reduce-scatter.2.cloned.1.call-update) | async-done | bytes 524304 | tf_op jit(solution)/shard_map/while/body/eval_jaxpr/reduce_scatter | solution.py:277
  1538.8 28.5 %moe_chunk.6 = f32[512,1024]{1,0:T(8,128)} custom-call(s32[15]{0:T(128)} %get-tuple-element.885.te_ref, s32[15]{0:T(128)} %get-tuple-element.886.tk_ref, s32[1]{0:T(128)} %get-tuple-element.976.first_ref, bf16[512,1024]{1,0:T(8,128)(2,1)} %all-gather.2.cloned.1.call-done.n_ref, s32[8,512]{1,0:T(8,128)} %dynamic-slice_bitcast_fusion.9.ids_ref, ...), custom_call_target="tpu_custom_call" | custom-call | flops 10000000000 | bytes 30000000 | tf_op jit(solution)/shard_map/while/body/eval_jaxpr/moe_chunk/pallas_call | solution.py:199
  1567.4 25.7 %reduce-scatter.2.cloned.1.call-done = f32[128,1024]{1,0:T(8,128)} async-done(((f32[512,1024]{1,0:T(8,128)}), f32[128,1024]{1,0:T(8,128)}) %reduce-scatter.2.cloned.1.call-update) | async-done | bytes 524304 | tf_op jit(solution)/shard_map/while/body/eval_jaxpr/reduce_scatter | solution.py:277
  1650.8 28.5 %moe_chunk.6 = f32[512,1024]{1,0:T(8,128)} custom-call(s32[15]{0:T(128)} %get-tuple-element.885.te_ref, s32[15]{0:T(128)} %get-tuple-element.886.tk_ref, s32[1]{0:T(128)} %get-tuple-element.976.first_ref, bf16[512,1024]{1,0:T(8,128)(2,1)} %all-gather.2.cloned.1.call-done.n_ref, s32[8,512]{1,0:T(8,128)} %dynamic-slice_bitcast_fusion.9.ids_ref, ...), custom_call_target="tpu_custom_call" | custom-call | flops 10000000000 | bytes 30000000 | tf_op jit(solution)/shard_map/while/body/eval_jaxpr/moe_chunk/pallas_call | solution.py:199
  1679.3 25.7 %reduce-scatter.2.cloned.1.call-done = f32[128,1024]{1,0:T(8,128)} async-done(((f32[512,1024]{1,0:T(8,128)}), f32[128,1024]{1,0:T(8,128)}) %reduce-scatter.2.cloned.1.call-update) | async-done | bytes 524304 | tf_op jit(solution)/shard_map/while/body/eval_jaxpr/reduce_scatter | solution.py:277
  1762.7 28.5 %moe_chunk.6 = f32[512,1024]{1,0:T(8,128)} custom-call(s32[15]{0:T(128)} %get-tuple-element.885.te_ref, s32[15]{0:T(128)} %get-tuple-element.886.tk_ref, s32[1]{0:T(128)} %get-tuple-element.976.first_ref, bf16[512,1024]{1,0:T(8,128)(2,1)} %all-gather.2.cloned.1.call-done.n_ref, s32[8,512]{1,0:T(8,128)} %dynamic-slice_bitcast_fusion.9.ids_ref, ...), custom_call_target="tpu_custom_call" | custom-call | flops 10000000000 | bytes 30000000 | tf_op jit(solution)/shard_map/while/body/eval_jaxpr/moe_chunk/pallas_call | solution.py:199
  1791.3 25.7 %reduce-scatter.2.cloned.1.call-done = f32[128,1024]{1,0:T(8,128)} async-done(((f32[512,1024]{1,0:T(8,128)}), f32[128,1024]{1,0:T(8,128)}) %reduce-scatter.2.cloned.1.call-update) | async-done | bytes 524304 | tf_op jit(solution)/shard_map/while/body/eval_jaxpr/reduce_scatter | solution.py:277
  1874.7 28.5 %moe_chunk.6 = f32[512,1024]{1,0:T(8,128)} custom-call(s32[15]{0:T(128)} %get-tuple-element.885.te_ref, s32[15]{0:T(128)} %get-tuple-element.886.tk_ref, s32[1]{0:T(128)} %get-tuple-element.976.first_ref, bf16[512,1024]{1,0:T(8,128)(2,1)} %all-gather.2.cloned.1.call-done.n_ref, s32[8,512]{1,0:T(8,128)} %dynamic-slice_bitcast_fusion.9.ids_ref, ...), custom_call_target="tpu_custom_call" | custom-call | flops 10000000000 | bytes 30000000 | tf_op jit(solution)/shard_map/while/body/eval_jaxpr/moe_chunk/pallas_call | solution.py:199
  1903.2 25.7 %reduce-scatter.2.cloned.1.call-done = f32[128,1024]{1,0:T(8,128)} async-done(((f32[512,1024]{1,0:T(8,128)}), f32[128,1024]{1,0:T(8,128)}) %reduce-scatter.2.cloned.1.call-update) | async-done | bytes 524304 | tf_op jit(solution)/shard_map/while/body/eval_jaxpr/reduce_scatter | solution.py:277
  1946.8 103.1 %all-reduce.2.cloned.1.call-done = bf16[64,32,1024]{2,1,0:T(8,128)(2,1)} async-done(((bf16[64,32,1024]{2,1,0:T(8,128)(2,1)}), bf16[64,32,1024]{2,1,0:T(8,128)(2,1)}) %all-reduce.2.cloned.1.call-update) | async-done | bytes 4194320 | tf_op jit(solution)/shard_map/psum | solution.py:290
  (597 shorter events, 841.1 us)
Async XLA Ops:
  37.3 46.3 %all-gather.2.cloned.1.call-start = ((), (), s32[]{:S(2)}) async-start(), calls=%async_computation.2 | async-start | bytes 1310720 | tf_op jit(solution)/shard_map/while/body/eval_jaxpr/all_gather | solution.py:275
  69.7 68.2 %reduce-scatter.2.cloned.1.call-start = ((), (), s32[]{:S(2)}) async-start(), calls=%async_computation.3 | async-start | bytes 2621440 | tf_op jit(solution)/shard_map/while/body/eval_jaxpr/reduce_scatter | solution.py:277
  148.3 47.3 %all-gather.2.cloned.1.call-start = ((), (), s32[]{:S(2)}) async-start(), calls=%async_computation.2 | async-start | bytes 1310720 | tf_op jit(solution)/shard_map/while/body/eval_jaxpr/all_gather | solution.py:275
  180.6 69.1 %reduce-scatter.2.cloned.1.call-start = ((), (), s32[]{:S(2)}) async-start(), calls=%async_computation.3 | async-start | bytes 2621440 | tf_op jit(solution)/shard_map/while/body/eval_jaxpr/reduce_scatter | solution.py:277
  251.6 8.6 collective-permute-start
  260.2 47.3 %all-gather.2.cloned.1.call-start = ((), (), s32[]{:S(2)}) async-start(), calls=%async_computation.2 | async-start | bytes 1310720 | tf_op jit(solution)/shard_map/while/body/eval_jaxpr/all_gather | solution.py:275
  292.6 69.1 %reduce-scatter.2.cloned.1.call-start = ((), (), s32[]{:S(2)}) async-start(), calls=%async_computation.3 | async-start | bytes 2621440 | tf_op jit(solution)/shard_map/while/body/eval_jaxpr/reduce_scatter | solution.py:277
  363.5 8.6 collective-permute-start
  372.2 47.3 %all-gather.2.cloned.1.call-start = ((), (), s32[]{:S(2)}) async-start(), calls=%async_computation.2 | async-start | bytes 1310720 | tf_op jit(solution)/shard_map/while/body/eval_jaxpr/all_gather | solution.py:275
  404.5 69.1 %reduce-scatter.2.cloned.1.call-start = ((), (), s32[]{:S(2)}) async-start(), calls=%async_computation.3 | async-start | bytes 2621440 | tf_op jit(solution)/shard_map/while/body/eval_jaxpr/reduce_scatter | solution.py:277
  475.5 8.6 collective-permute-start
  484.1 47.3 %all-gather.2.cloned.1.call-start = ((), (), s32[]{:S(2)}) async-start(), calls=%async_computation.2 | async-start | bytes 1310720 | tf_op jit(solution)/shard_map/while/body/eval_jaxpr/all_gather | solution.py:275
  516.5 69.1 %reduce-scatter.2.cloned.1.call-start = ((), (), s32[]{:S(2)}) async-start(), calls=%async_computation.3 | async-start | bytes 2621440 | tf_op jit(solution)/shard_map/while/body/eval_jaxpr/reduce_scatter | solution.py:277
  596.0 47.3 %all-gather.2.cloned.1.call-start = ((), (), s32[]{:S(2)}) async-start(), calls=%async_computation.2 | async-start | bytes 1310720 | tf_op jit(solution)/shard_map/while/body/eval_jaxpr/all_gather | solution.py:275
  628.4 69.1 %reduce-scatter.2.cloned.1.call-start = ((), (), s32[]{:S(2)}) async-start(), calls=%async_computation.3 | async-start | bytes 2621440 | tf_op jit(solution)/shard_map/while/body/eval_jaxpr/reduce_scatter | solution.py:277
  699.3 8.6 collective-permute-start
  708.0 47.3 %all-gather.2.cloned.1.call-start = ((), (), s32[]{:S(2)}) async-start(), calls=%async_computation.2 | async-start | bytes 1310720 | tf_op jit(solution)/shard_map/while/body/eval_jaxpr/all_gather | solution.py:275
  740.3 69.1 %reduce-scatter.2.cloned.1.call-start = ((), (), s32[]{:S(2)}) async-start(), calls=%async_computation.3 | async-start | bytes 2621440 | tf_op jit(solution)/shard_map/while/body/eval_jaxpr/reduce_scatter | solution.py:277
  811.3 8.6 collective-permute-start
  819.9 47.3 %all-gather.2.cloned.1.call-start = ((), (), s32[]{:S(2)}) async-start(), calls=%async_computation.2 | async-start | bytes 1310720 | tf_op jit(solution)/shard_map/while/body/eval_jaxpr/all_gather | solution.py:275
  852.3 69.1 %reduce-scatter.2.cloned.1.call-start = ((), (), s32[]{:S(2)}) async-start(), calls=%async_computation.3 | async-start | bytes 2621440 | tf_op jit(solution)/shard_map/while/body/eval_jaxpr/reduce_scatter | solution.py:277
  923.2 8.6 collective-permute-start
  931.9 47.3 %all-gather.2.cloned.1.call-start = ((), (), s32[]{:S(2)}) async-start(), calls=%async_computation.2 | async-start | bytes 1310720 | tf_op jit(solution)/shard_map/while/body/eval_jaxpr/all_gather | solution.py:275
  964.2 69.1 %reduce-scatter.2.cloned.1.call-start = ((), (), s32[]{:S(2)}) async-start(), calls=%async_computation.3 | async-start | bytes 2621440 | tf_op jit(solution)/shard_map/while/body/eval_jaxpr/reduce_scatter | solution.py:277
  1035.2 8.6 collective-permute-start
  1043.8 47.3 %all-gather.2.cloned.1.call-start = ((), (), s32[]{:S(2)}) async-start(), calls=%async_computation.2 | async-start | bytes 1310720 | tf_op jit(solution)/shard_map/while/body/eval_jaxpr/all_gather | solution.py:275
  1076.2 69.1 %reduce-scatter.2.cloned.1.call-start = ((), (), s32[]{:S(2)}) async-start(), calls=%async_computation.3 | async-start | bytes 2621440 | tf_op jit(solution)/shard_map/while/body/eval_jaxpr/reduce_scatter | solution.py:277
  1147.1 8.6 collective-permute-start
  1155.8 47.3 %all-gather.2.cloned.1.call-start = ((), (), s32[]{:S(2)}) async-start(), calls=%async_computation.2 | async-start | bytes 1310720 | tf_op jit(solution)/shard_map/while/body/eval_jaxpr/all_gather | solution.py:275
  1188.1 69.1 %reduce-scatter.2.cloned.1.call-start = ((), (), s32[]{:S(2)}) async-start(), calls=%async_computation.3 | async-start | bytes 2621440 | tf_op jit(solution)/shard_map/while/body/eval_jaxpr/reduce_scatter | solution.py:277
  1259.1 8.6 collective-permute-start
  1267.7 47.3 %all-gather.2.cloned.1.call-start = ((), (), s32[]{:S(2)}) async-start(), calls=%async_computation.2 | async-start | bytes 1310720 | tf_op jit(solution)/shard_map/while/body/eval_jaxpr/all_gather | solution.py:275
  1300.0 69.1 %reduce-scatter.2.cloned.1.call-start = ((), (), s32[]{:S(2)}) async-start(), calls=%async_computation.3 | async-start | bytes 2621440 | tf_op jit(solution)/shard_map/while/body/eval_jaxpr/reduce_scatter | solution.py:277
  1371.0 8.6 collective-permute-start
  1379.6 47.3 %all-gather.2.cloned.1.call-start = ((), (), s32[]{:S(2)}) async-start(), calls=%async_computation.2 | async-start | bytes 1310720 | tf_op jit(solution)/shard_map/while/body/eval_jaxpr/all_gather | solution.py:275
  1412.0 69.1 %reduce-scatter.2.cloned.1.call-start = ((), (), s32[]{:S(2)}) async-start(), calls=%async_computation.3 | async-start | bytes 2621440 | tf_op jit(solution)/shard_map/while/body/eval_jaxpr/reduce_scatter | solution.py:277
  1491.6 47.3 %all-gather.2.cloned.1.call-start = ((), (), s32[]{:S(2)}) async-start(), calls=%async_computation.2 | async-start | bytes 1310720 | tf_op jit(solution)/shard_map/while/body/eval_jaxpr/all_gather | solution.py:275
  1523.9 69.1 %reduce-scatter.2.cloned.1.call-start = ((), (), s32[]{:S(2)}) async-start(), calls=%async_computation.3 | async-start | bytes 2621440 | tf_op jit(solution)/shard_map/while/body/eval_jaxpr/reduce_scatter | solution.py:277
  1594.9 8.6 collective-permute-start
  1603.5 47.3 %all-gather.2.cloned.1.call-start = ((), (), s32[]{:S(2)}) async-start(), calls=%async_computation.2 | async-start | bytes 1310720 | tf_op jit(solution)/shard_map/while/body/eval_jaxpr/all_gather | solution.py:275
  1635.9 69.1 %reduce-scatter.2.cloned.1.call-start = ((), (), s32[]{:S(2)}) async-start(), calls=%async_computation.3 | async-start | bytes 2621440 | tf_op jit(solution)/shard_map/while/body/eval_jaxpr/reduce_scatter | solution.py:277
  1706.8 8.6 collective-permute-start
  1715.5 47.3 %all-gather.2.cloned.1.call-start = ((), (), s32[]{:S(2)}) async-start(), calls=%async_computation.2 | async-start | bytes 1310720 | tf_op jit(solution)/shard_map/while/body/eval_jaxpr/all_gather | solution.py:275
  1747.8 69.1 %reduce-scatter.2.cloned.1.call-start = ((), (), s32[]{:S(2)}) async-start(), calls=%async_computation.3 | async-start | bytes 2621440 | tf_op jit(solution)/shard_map/while/body/eval_jaxpr/reduce_scatter | solution.py:277
  1827.4 47.3 %all-gather.2.cloned.1.call-start = ((), (), s32[]{:S(2)}) async-start(), calls=%async_computation.2 | async-start | bytes 1310720 | tf_op jit(solution)/shard_map/while/body/eval_jaxpr/all_gather | solution.py:275
  1859.7 69.1 %reduce-scatter.2.cloned.1.call-start = ((), (), s32[]{:S(2)}) async-start(), calls=%async_computation.3 | async-start | bytes 2621440 | tf_op jit(solution)/shard_map/while/body/eval_jaxpr/reduce_scatter | solution.py:277
  1930.7 8.6 collective-permute-start
  1939.3 110.6 %all-reduce.2.cloned.1.call-start = ((), (), s32[]{:S(2)}) async-start(), calls=%async_computation.1 | async-start | bytes 8388608 | tf_op jit(solution)/shard_map/psum | solution.py:290
  (77 other events, 3155.5 us)
Sparse Core Ops, SparseCore 0:
  69.8 13.7 all-gather.1
  112.3 25.5 reduce-scatter.1
  180.8 14.7 all-gather.1
  224.2 25.5 reduce-scatter.1
  292.7 14.7 all-gather.1
  336.1 25.5 reduce-scatter.1
  404.6 14.7 all-gather.1
  448.1 25.5 reduce-scatter.1
  516.6 14.7 all-gather.1
  560.0 25.5 reduce-scatter.1
  628.5 14.7 all-gather.1
  672.0 25.5 reduce-scatter.1
  740.5 14.7 all-gather.1
  783.9 25.5 reduce-scatter.1
  852.4 14.7 all-gather.1
  895.8 25.5 reduce-scatter.1
  964.3 14.7 all-gather.1
  1007.8 25.5 reduce-scatter.1
  1076.3 14.7 all-gather.1
  1119.7 25.5 reduce-scatter.1
  1188.2 14.7 all-gather.1
  1231.7 25.5 reduce-scatter.1
  1300.2 14.7 all-gather.1
  1343.6 25.5 reduce-scatter.1
  1412.1 14.7 all-gather.1
  1455.6 25.5 reduce-scatter.1
  1524.0 14.7 all-gather.1
  1567.5 25.5 reduce-scatter.1
  1636.0 14.7 all-gather.1
  1679.4 25.5 reduce-scatter.1
  1747.9 14.7 all-gather.1
  1791.4 25.5 reduce-scatter.1
  1859.9 14.7 all-gather.1
  1903.3 25.5 reduce-scatter.1
Sparse Core Ops, SparseCore 1:
  1946.9 103.0 all-reduce.1

commit v2 on v1

v2 whole, which is shorter than its diff:
```python
import functools

import jax
import jax.numpy as jnp
from jax import lax
from jax.experimental import pallas as pl
from jax.experimental.pallas import tpu as pltpu
from jax.sharding import PartitionSpec as P

THETA = 1000000.0
EPS = 1e-05
F32 = jnp.float32
BF16 = jnp.bfloat16
TILE = 128
GROUP = 16
PER_CHUNK = 4
HIN_SLOTS = 4
MESH = pl.DeviceIdType.MESH


def rms(vals, gain_row):
    inv = lax.rsqrt(jnp.mean(vals * vals, axis=-1, keepdims=True) + EPS)
    return (vals * inv * gain_row).astype(BF16)


def dot(lhs, rhs):
    return jnp.dot(lhs, rhs, preferred_element_type=F32)


def dot_nt(lhs, rhs):
    return lax.dot_general(lhs, rhs, (((1,), (1,)), ((), ())), preferred_element_type=F32)


def rope_table(pos, table_ref):
    picked = jnp.zeros(pos.shape, F32)
    for t in range(table_ref.shape[0]):
        picked = jnp.where(pos == t + 1, table_ref[t:t + 1, :], picked)
    return picked


def rope(vals, cos_t, sin_t):
    lane = lax.broadcasted_iota(jnp.int32, (1, 128), 1)
    first = (lane % 64) < 32
    parts = []
    for j in range(vals.shape[1] // 128):
        block = vals[:, j * 128:(j + 1) * 128]
        swapped = jnp.where(first, pltpu.roll(block, 96, 1), pltpu.roll(block, 32, 1))
        parts.append(block * cos_t + swapped * sin_t)
    return jnp.concatenate(parts, axis=1)


def dup_heads(vals):
    low = lax.broadcasted_iota(jnp.int32, (1, 128), 1) < 64
    parts = []
    for j in range(vals.shape[1] // 128):
        block = vals[:, j * 128:(j + 1) * 128]
        other = pltpu.roll(block, 64, 1)
        parts.append(jnp.where(low, block, other))
        parts.append(jnp.where(low, other, block))
    return jnp.concatenate(parts, axis=1)


def attn_project(hidden, pos, w, q3, k3, v3):
    tokens = hidden.shape[0]
    normed = rms(hidden.astype(F32), w["a_gain"][...].astype(F32))
    cos_t = rope_table(pos, w["cos"])
    sin_t = rope_table(pos, w["sin"])
    q = rope(dot(normed, w["q"][...]).astype(BF16).astype(F32), cos_t, sin_t)
    q3[...] = q.astype(BF16).astype(F32).reshape(tokens, -1, 128)
    k = rope(dot(normed, w["k"][...]).astype(BF16).astype(F32), cos_t, sin_t)
    k3[...] = dup_heads(k.astype(BF16).astype(F32)).reshape(tokens, -1, 128)
    v3[...] = dup_heads(dot(normed, w["v"][...]).astype(BF16).astype(F32)).reshape(tokens, -1, 128)


def attn_group(idx, q3, k3, v3, o3, pos_ref, k_rows, v_rows):
    base = pl.multiple_of(idx * GROUP, GROUP)
    span = pl.ds(base, GROUP)
    q = q3[span]
    lane3 = lax.broadcasted_iota(jnp.int32, (1, 1, 128), 2)
    prod = q * k3[span]
    self_a = jnp.sum(jnp.where(lane3 < 64, prod, 0.0), axis=-1, keepdims=True)
    self_b = jnp.sum(jnp.where(lane3 < 64, 0.0, prod), axis=-1, keepdims=True)
    self_s = jnp.concatenate([self_a, self_b], axis=1) * 0.125
    q_rows = jnp.concatenate([q, pltpu.roll(q, 64, 2)], axis=1).astype(BF16)[:, :, :64].reshape(GROUP * 16, 64)
    row0 = idx * (GROUP * 128)
    blocks = []
    for p in range(GROUP // 2):
        keys = k_rows[pl.ds(pl.multiple_of(row0 + p * 256, 256), 256), :]
        both = dot_nt(q_rows[p * 32:(p + 1) * 32], keys)
        blocks.append(both[:16, :128].reshape(1, 16, 128))
        blocks.append(both[16:, 128:].reshape(1, 16, 128))
    scores = jnp.concatenate(blocks, axis=0)
    row_i = lax.broadcasted_iota(jnp.int32, (16, 128), 0)
    lane_i = lax.broadcasted_iota(jnp.int32, (16, 128), 1)
    step = jnp.where((row_i % 8) == (lane_i % 8), lane_i // 8, 1000)
    pos = pos_ref[span, :].reshape(GROUP, 1, 128)
    scores = jnp.where(step.reshape(1, 16, 128) < pos, scores * 0.125, -jnp.inf)
    top = jnp.maximum(jnp.max(scores, axis=-1, keepdims=True), self_s)
    weights = jnp.exp(scores - top)
    self_w = jnp.exp(self_s - top)
    inv = 1.0 / (jnp.sum(weights, axis=-1, keepdims=True) + self_w)
    weights = (weights * inv).astype(BF16)
    self_w = (self_w * inv).astype(BF16).astype(F32)
    zeros = jnp.zeros((16, 128), BF16)
    outs = []
    for p in range(GROUP // 2):
        vals = v_rows[pl.ds(pl.multiple_of(row0 + p * 256, 256), 256), :]
        upper = jnp.concatenate([weights[2 * p], zeros], axis=1)
        lower = jnp.concatenate([zeros, weights[2 * p + 1]], axis=1)
        outs.append(dot(jnp.concatenate([upper, lower], axis=0), vals).reshape(2, 16, 64))
    out = jnp.concatenate(outs, axis=0)
    v_new = v3[span][:, :, :64]
    out_a = out[:, :8] + self_w[:, :8] * v_new
    out_b = out[:, 8:] + self_w[:, 8:] * v_new
    o3[span] = jnp.concatenate([out_a, out_b], axis=-1)


def moe_route(ids, normed, w_r, tri, rank_ref, gate_ref):
    tokens = ids.shape[1]
    expert_i = lax.broadcasted_iota(jnp.int32, (32, tokens), 0)
    chosen = jnp.zeros((32, tokens), F32)
    for s in range(ids.shape[0]):
        chosen = jnp.where(ids[s:s + 1, :] == expert_i, 1.0, chosen)
    rank = dot(chosen.astype(BF16), tri[...])
    rank_ref[...] = jnp.where(chosen > 0.0, rank, -1.0)
    logits = dot_nt(w_r[...], normed)
    top = jnp.max(jnp.where(chosen > 0.0, logits, -jnp.inf), axis=0, keepdims=True)
    gates = jnp.where(chosen > 0.0, jnp.exp(logits - top), 0.0)
    gate_ref[...] = gates / jnp.sum(gates, axis=0, keepdims=True)


def moe_tile(idx, expert, sub, first, normed, rank_ref, gate_ref, w, picks, terms):
    ranks = rank_ref[pl.ds(first + expert, 1), :]
    wanted = (lax.broadcasted_iota(jnp.int32, (TILE, 1), 0) + sub * TILE).astype(F32)
    picked = jnp.where(ranks == wanted, 1.0, 0.0)
    gate = jnp.sum(picked * gate_ref[pl.ds(first + expert, 1), :], axis=-1, keepdims=True)
    at = pl.ds(pl.multiple_of(idx * TILE, TILE), TILE)
    picks[:, at] = picked.T.astype(BF16)
    rows = dot(picked.astype(BF16), normed[...]).astype(BF16)
    act = jax.nn.silu(dot(rows, w["gate"][expert])) * dot(rows, w["up"][expert])
    terms[at, :] = (gate * dot(act.astype(BF16), w["down"][expert])).astype(BF16)


def step_kernel(
    tile_count,
    te_ref, tk_ref, hid, pos, k_cache, v_cache, ids, wq_h, wk_h, wv_h, wo_h, a_gain, m_gain, f_gain, cos_ref, sin_ref, w_r, wg_h, wu_h, wd_h, tri,
    out, kn_out, vn_out,
    n_buf, hin, mid, ho, k_buf, v_buf, wq, wk, wv, wo, wg, wu, wd, part, own, xsum, rb1, rb2, picks, terms, q3, k3, v3, o3, kn, vn, rank_ref, gate_ref,
    w_sem, hin_sem, kv_sem, new_sem, dx_send, dx_recv, dc_send, dc_recv, dr_send, dr_recv, r1_send, r1_recv, r2_send, r2_recv, hop_send, out_loc, out_recv, credit,
):
    chunks, tokens = hid.shape[0], hid.shape[1]
    gathered = 4 * tokens
    dp = lax.axis_index("dp")
    pp = lax.axis_index("pp")
    ep = lax.axis_index("ep")
    other_pp = (dp, 1 - pp, ep)
    across = (dp, pp, lax.rem(ep + 2, 4))
    beside = (dp, pp, ep + 1 - 2 * lax.rem(ep, 2))
    first = ep * 8

    barrier = pltpu.get_barrier_semaphore()
    for peer in (other_pp, across, beside):
        pl.semaphore_signal(barrier, inc=1, device_id=peer, device_id_type=MESH)
    pl.semaphore_wait(barrier, 3)

    attn_w = [(wq_h, wq), (wk_h, wk), (wv_h, wv), (wo_h, wo)]
    moe_w = [(wg_h, wg), (wu_h, wu), (wd_h, wd)]
    weight_copies = [pltpu.make_async_copy(s, d, w_sem.at[j]) for j, (s, d) in enumerate(attn_w + moe_w)]

    def hin_copy(c):
        return pltpu.make_async_copy(hid.at[c], hin.at[lax.rem(c, HIN_SLOTS)], hin_sem.at[lax.rem(c, HIN_SLOTS)])

    def kv_copies(c):
        return (pltpu.make_async_copy(k_cache.at[c], k_buf, kv_sem.at[0]), pltpu.make_async_copy(v_cache.at[c], v_buf, kv_sem.at[1]))

    def new_copies(c):
        return (pltpu.make_async_copy(kn, kn_out.at[c], new_sem.at[0]), pltpu.make_async_copy(vn, vn_out.at[c], new_sem.at[1]))

    def remote(src, dst, send, recv, peer):
        return pltpu.make_async_remote_copy(src_ref=src, dst_ref=dst, send_sem=send, recv_sem=recv, device_id=peer, device_id_type=MESH)

    def rows_at(slot, part_idx):
        return n_buf.at[slot, pl.ds(part_idx * tokens, tokens)]

    def dx_copy(c):
        s = lax.rem(c, 3)
        return remote(rows_at(s, 0), rows_at(s, 1), dx_send.at[s], dx_recv.at[s], across)

    def dc_copy(c):
        s = lax.rem(c, 3)
        return remote(rows_at(s, 0), rows_at(s, 2), dc_send.at[s], dc_recv.at[s], beside)

    def dr_copy(c):
        s = lax.rem(c, 3)
        return remote(rows_at(s, 1), rows_at(s, 3), dr_send.at[s], dr_recv.at[s], beside)

    def r1_copy(c):
        s = lax.rem(c, 2)
        return remote(part.at[pl.ds(2 * tokens, 2 * tokens)], rb1.at[s], r1_send.at[s], r1_recv.at[s], beside)

    def r2_copy(c):
        s = lax.rem(c, 3)
        return remote(xsum, rb2.at[s], r2_send.at[s], r2_recv.at[s], across)

    def hop_copy(c):
        s = lax.rem(c, 2)
        h = lax.rem(c, HIN_SLOTS)
        return remote(ho.at[s], hin.at[h], hop_send.at[s], hin_sem.at[h], other_pp)

    def out_copy(c):
        s = lax.rem(c, 2)
        return remote(ho.at[s], out.at[c], hop_send.at[s], out_recv.at[c], other_pp)

    def out_local(c):
        s = lax.rem(c, 2)
        return pltpu.make_async_copy(ho.at[s], out.at[c], out_loc.at[s])

    for copy in weight_copies[:3]:
        copy.start()

    @pl.when(pp == 0)
    def _():
        hin_copy(0).start()

    for copy in kv_copies(0):
        copy.start()
    for copy in weight_copies[3:]:
        copy.start()

    @pl.when(pp == 0)
    def _():
        hin_copy(1).start()

    w = {"a_gain": a_gain, "cos": cos_ref, "sin": sin_ref, "q": wq, "k": wk, "v": wv, "gate": wg, "up": wu, "down": wd}

    def project(c):
        hin_copy(c).wait()

        @pl.when(c == 0)
        def _():
            for copy in weight_copies[:3]:
                copy.wait()

        @pl.when(jnp.logical_and(pp == 0, c + 2 < chunks))
        def _():
            hin_copy(c + 2).start()

        @pl.when(c > 0)
        def _():
            for copy in new_copies(c - 1):
                copy.wait()

        attn_project(hin[lax.rem(c, HIN_SLOTS)], pos[c], w, q3, k3, v3)
        kn[...] = k3[...][:, :, :64].astype(BF16)
        vn[...] = v3[...][:, :, :64].astype(BF16)
        for copy in new_copies(c):
            copy.start()

    def reduce_pair(c):
        copy = r1_copy(c)
        copy.wait_send()
        copy.wait_recv()
        s = lax.rem(c, 2)
        xsum[...] = part[pl.ds(tokens, tokens), :] + rb1[s, pl.ds(tokens, tokens), :]
        r2_copy(c).start()
        own[...] = part[pl.ds(0, tokens), :] + rb1[s, pl.ds(0, tokens), :]

    def relay(c):
        copy = dx_copy(c)
        copy.wait_recv()
        dr_copy(c).start()
        copy.wait_send()
        dc_copy(c).wait_send()

    def attend(c):
        for copy in kv_copies(c):
            copy.wait()

        def body(idx, carry):
            attn_group(idx, q3, k3, v3, o3, pos.at[c], k_buf, v_buf)
            return carry

        lax.fori_loop(0, tokens // GROUP, body, 0)

        @pl.when(c + 1 < chunks)
        def _():
            for copy in kv_copies(c + 1):
                copy.start()

        @pl.when(c == 0)
        def _():
            weight_copies[3].wait()

        hidden = hin[lax.rem(c, HIN_SLOTS)].astype(F32)
        attn_out = o3[...].reshape(tokens, 1024).astype(BF16)
        new_mid = (hidden + dot(attn_out, wo[...])).astype(BF16)
        mid[lax.rem(c, 3)] = new_mid
        n_buf[lax.rem(c, 3), pl.ds(0, tokens), :] = rms(new_mid.astype(F32), m_gain[...].astype(F32))
        dx_copy(c).start()
        dc_copy(c).start()

        @pl.when(jnp.logical_and(pp == 1, c + HIN_SLOTS < chunks))
        def _():
            pl.semaphore_signal(credit, inc=1, device_id=other_pp, device_id_type=MESH)

    def experts(c):
        s = lax.rem(c, 3)
        dc_copy(c).wait_recv()
        relayed = dr_copy(c)
        relayed.wait_recv()
        normed = n_buf.at[s]
        moe_route(ids[c], normed[...], w_r, tri, rank_ref, gate_ref)

        @pl.when(c == 0)
        def _():
            for copy in weight_copies[4:]:
                copy.wait()

        def body(idx, carry):
            moe_tile(idx, te_ref[c, idx], tk_ref[c, idx], first, normed, rank_ref, gate_ref, w, picks, terms)
            return carry

        lax.fori_loop(0, tile_count, body, 0)

        def combine(idx, carry):
            cols = pl.ds(pl.multiple_of(idx * 256, 256), 256)
            part[:, cols] = dot(picks[...], terms[:, cols])
            return carry

        lax.fori_loop(0, 4, combine, 0)
        relayed.wait_send()
        r1_copy(c).start()

    def finish(c):
        s = lax.rem(c, 2)
        copy = r2_copy(c)
        copy.wait_recv()
        copy.wait_send()
        mixed = (own[...] + rb2[lax.rem(c, 3)]).astype(BF16)
        result = (mid[lax.rem(c, 3)].astype(F32) + mixed.astype(F32)).astype(BF16)

        @pl.when(pp == 0)
        def _():
            @pl.when(c >= 2)
            def _():
                hop_copy(c - 2).wait_send()

            @pl.when(c >= HIN_SLOTS)
            def _():
                pl.semaphore_wait(credit, 1)

            ho[s] = result
            hop_copy(c).start()

        @pl.when(pp == 1)
        def _():
            @pl.when(c >= 2)
            def _():
                out_copy(c - 2).wait_send()
                out_local(c - 2).wait()

            ho[s] = rms(result.astype(F32), f_gain[...].astype(F32))
            out_copy(c).start()
            out_local(c).start()

    def step(i, carry):
        @pl.when(i < chunks)
        def _():
            project(i)

        @pl.when(jnp.logical_and(i >= 1, i <= chunks))
        def _():
            relay(i - 1)

        @pl.when(i >= 2)
        def _():
            reduce_pair(i - 2)

        @pl.when(i < chunks)
        def _():
            attend(i)

        @pl.when(jnp.logical_and(i >= 1, i <= chunks))
        def _():
            experts(i - 1)

        @pl.when(i >= 2)
        def _():
            finish(i - 2)

        return carry

    lax.fori_loop(0, chunks + 2, step, 0)

    for copy in new_copies(chunks - 1):
        copy.wait()

    @pl.when(pp == 0)
    def _():
        for c in (chunks - 2, chunks - 1):
            hop_copy(c).wait_send()

        def arrived(c, carry):
            out_copy(c).wait_recv()
            return carry

        lax.fori_loop(0, chunks, arrived, 0)

    @pl.when(pp == 1)
    def _():
        for c in (chunks - 2, chunks - 1):
            out_copy(c).wait_send()
            out_local(c).wait()


def step_call(args, chunks, tokens, tile_count):
    vmem = pl.BlockSpec(memory_space=pltpu.VMEM)
    smem = pl.BlockSpec(memory_space=pltpu.SMEM)
    hbm = pl.BlockSpec(memory_space=pl.ANY)
    wide = 4 * tokens
    dma = pltpu.SemaphoreType.DMA
    return pl.pallas_call(
        functools.partial(step_kernel, tile_count),
        out_shape=(
            jax.ShapeDtypeStruct((chunks, tokens, 1024), BF16),
            jax.ShapeDtypeStruct((chunks, tokens, 8, 64), BF16),
            jax.ShapeDtypeStruct((chunks, tokens, 8, 64), BF16),
        ),
        in_specs=[smem, smem, hbm, vmem, hbm, hbm, vmem, hbm, hbm, hbm, hbm, vmem, vmem, vmem, vmem, vmem, vmem, hbm, hbm, hbm, vmem],
        out_specs=(hbm, hbm, hbm),
        scratch_shapes=[
            pltpu.VMEM((3, wide, 1024), BF16),
            pltpu.VMEM((HIN_SLOTS, tokens, 1024), BF16),
            pltpu.VMEM((3, tokens, 1024), BF16),
            pltpu.VMEM((2, tokens, 1024), BF16),
            pltpu.VMEM((tokens * 128, 64), BF16),
            pltpu.VMEM((tokens * 128, 64), BF16),
            pltpu.VMEM((1024, 1024), BF16),
            pltpu.VMEM((1024, 512), BF16),
            pltpu.VMEM((1024, 512), BF16),
            pltpu.VMEM((1024, 1024), BF16),
            pltpu.VMEM((8, 1024, 512), BF16),
            pltpu.VMEM((8, 1024, 512), BF16),
            pltpu.VMEM((8, 512, 1024), BF16),
            pltpu.VMEM((wide, 1024), F32),
            pltpu.VMEM((tokens, 1024), F32),
            pltpu.VMEM((tokens, 1024), F32),
            pltpu.VMEM((2, 2 * tokens, 1024), F32),
            pltpu.VMEM((3, tokens, 1024), F32),
            pltpu.VMEM((wide, tile_count * TILE), BF16),
            pltpu.VMEM((tile_count * TILE, 1024), BF16),
            pltpu.VMEM((tokens, 8, 128), F32),
            pltpu.VMEM((tokens, 8, 128), F32),
            pltpu.VMEM((tokens, 8, 128), F32),
            pltpu.VMEM((tokens, 8, 128), F32),
            pltpu.VMEM((tokens, 8, 64), BF16),
            pltpu.VMEM((tokens, 8, 64), BF16),
            pltpu.VMEM((32, wide), F32),
            pltpu.VMEM((32, wide), F32),
            dma((7,)), dma((HIN_SLOTS,)), dma((2,)), dma((2,)),
            dma((3,)), dma((3,)), dma((3,)), dma((3,)), dma((3,)), dma((3,)),
            dma((2,)), dma((2,)), dma((3,)), dma((3,)),
            dma((2,)), dma((2,)), dma((chunks,)),
            pltpu.SemaphoreType.REGULAR,
        ],
        compiler_params=pltpu.CompilerParams(collective_id=0, has_side_effects=True, vmem_limit_bytes=67043328),
        name="decode_step",
        cost_estimate=pl.CostEstimate(flops=2 * 10**11, bytes_accessed=2 * 10**8, transcendentals=0),
    )(*args)


def tile_tables(ids, first, tile_count):
    local = first + jnp.arange(8, dtype=jnp.int32)
    counts = jnp.sum((ids[:, None] == local[None, :, None, None]).astype(jnp.int32), axis=(2, 3))
    tiles = (counts + TILE - 1) // TILE
    ends = jnp.cumsum(tiles, axis=1)
    idx = jnp.arange(tile_count, dtype=jnp.int32)
    expert = jnp.sum((idx[None, :, None] >= ends[:, None, :]).astype(jnp.int32), axis=-1)
    safe = jnp.minimum(expert, 7)
    starts = ends - tiles
    start = jnp.sum(jnp.where(safe[:, :, None] == jnp.arange(8)[None, None, :], starts[:, None, :], 0), axis=-1)
    sub = jnp.where(expert < 8, idx[None, :] - start, 1000)
    return safe, sub.astype(jnp.int32)


def solution(mesh):
    rows_spec = ("dp", "ep")
    three_dim = P("pp", None, None)
    two_dim = P("pp", None)
    expert_spec = P("pp", "ep", None, None)
    cache_spec = P("pp", None, rows_spec, None, None, None)
    new_spec = P("pp", None, rows_spec, None, None)
    in_specs = (P(None, rows_spec, None), P(None, rows_spec), cache_spec, cache_spec, P("pp", None, rows_spec, None), three_dim, three_dim, three_dim, three_dim, two_dim, two_dim, three_dim, expert_spec, expert_spec, expert_spec, P(None))
    out_specs = (P(None, rows_spec, None), new_spec, new_spec)

    def device_fn(hidden_in, seq_pos, k_cache, v_cache, expert_ids, w_query, w_key, w_value, w_out, attn_gain, mlp_gain, w_router, w_gate, w_up, w_down, final_gain):
        ep_idx = lax.axis_index("ep")
        micro, rows = seq_pos.shape
        chunks = micro // PER_CHUNK
        tokens = PER_CHUNK * rows
        wide = 4 * tokens
        tile_count = (wide * 2 - 8) // TILE + 8
        pos = jnp.broadcast_to(seq_pos.reshape(micro * rows, 1), (micro * rows, 128)).reshape(chunks, tokens, 128)
        angles = jnp.arange(1, 17, dtype=F32)[:, None] * THETA ** (-jnp.arange(32, dtype=F32) / 32)
        cos_t = jnp.tile(jnp.cos(angles), (1, 4))
        sin_t = jnp.tile(jnp.concatenate([-jnp.sin(angles), jnp.sin(angles)], axis=1), (1, 2))
        beside = ep_idx + 1 - 2 * (ep_idx % 2)
        order = jnp.stack([ep_idx, (ep_idx + 2) % 4, beside, (beside + 2) % 4])
        ids = lax.all_gather(expert_ids[0].reshape(chunks, tokens, 8), "ep", axis=0, tiled=False)
        ids = jnp.transpose(ids[order], (1, 3, 0, 2)).reshape(chunks, 8, wide)
        te, tk = tile_tables(ids, ep_idx * 8, tile_count)
        ti = jnp.arange(wide)
        tri = (ti[:, None] < ti[None, :]).astype(BF16)
        args = (
            te, tk, hidden_in.reshape(chunks, tokens, 1024), pos, k_cache.reshape(chunks, tokens * 128, 64), v_cache.reshape(chunks, tokens * 128, 64),
            ids, w_query[0], w_key[0], w_value[0], w_out[0], attn_gain, mlp_gain, final_gain.reshape(1, -1), cos_t, sin_t, w_router[0].T,
            w_gate[0], w_up[0], w_down[0], tri,
        )
        out, k_new, v_new = step_call(args, chunks, tokens, tile_count)
        shape = (1,) + seq_pos.shape + (8, 64)
        return out.reshape(hidden_in.shape), k_new.reshape(shape), v_new.reshape(shape)

    return jax.shard_map(device_fn, mesh=mesh, in_specs=in_specs, out_specs=out_specs, check_vma=False)
```

time: 2070 us -> 585 us (0.28)
  waiting for transfers between devices: 810 us -> 0 us
  local copies, waits for them, and re-layouts: 343 us -> 19 us
  Pallas kernels: 740 us -> 550 us
  other arithmetic: 84.2 us -> 4.41 us
  starting transfers between devices: 58 us -> 0 us
    reduce_scatter x17 -> x0, waiting for transfers between devices: 437 us -> none  [tick(): lax.psum_scatter(part, 'ep', scatter_dimension=0, tiled=True).astype(BF16)]
    all_gather x17 -> x0, waiting for transfers between devices: 205 us -> none  [tick(): n_all = lax.all_gather(normed, 'ep', axis=0, tiled=True)]
    pallas_call x34 -> x1, Pallas kernels: 740 us -> 550 us  [step_call(): pl.pallas_call(functools.partial(step_kernel, tile_count), out_shape=(jax...]
    squeeze x68 -> x0, local copies, waits for them, and re-layouts: 157 us -> none  [tick(): at = lambda arr: lax.dynamic_index_in_dim(arr, c, 0, keepdims=False)]
    psum x1 -> x0, waiting for transfers between devices: 103 us -> none  [device_fn(): return (lax.psum(final, 'pp'), k_buf.reshape(shape), v_buf.reshape(shape))]
    reshape x34 -> x1, local copies, waits for them, and re-layouts: 87.8 us -> 1.28 us  [device_fn(): final_gain.reshape(1, -1)]
    ppermute x17 -> x0, waiting for transfers between devices: 64.7 us -> none  [tick(): return (lax.ppermute(result, 'pp', shift_perm), out_buf, k_buf, v_buf)]
    ppermute x17 -> x0, starting transfers between devices: 57.2 us -> none  [tick(): return (lax.ppermute(result, 'pp', shift_perm), out_buf, k_buf, v_buf)]
  transfers between devices with their start and end apart: 52 -> 0, of which waited for: 52 -> 0; matrix products, arithmetic and copies ran while one was open for 3% -> 0% of each run, Pallas kernels for 0% -> 0%
where the time goes in v2:
time: 585 us
  Pallas kernels  550 us (94%)
  local copies, waits for them, and re-layouts  19 us (3%)
  blocking collectives  10.8 us (2%)
    pallas_call x1, Pallas kernels, step_call(): pl.pallas_call(functools.partial(step_kernel, tile_count), out_shape=(jax...  550 us
    unnamed x13, local copies, waits for them, and re-layouts  13.9 us

profile of v2, /device:TPU:0, one launch (start us, length us, event | category | flops | bytes accessed | tf_op | source)
XLA Modules:
  0.0 585.0 jit_solution(11111441375815478086)
XLA Ops:
  0.7 0.1 fusion.4
  0.8 1.3 reshape.274.f_gain
  2.1 0.1 fusion.3
  2.2 0.1 pad_maximum_fusion
  2.3 0.7 tile.21.sin_ref
  3.0 0.7 tile.9.cos_ref
  3.6 0.8 copy.36
  4.4 0.1 broadcast_in_dim.23
  4.5 1.0 copy.27
  5.5 0.1 all_gather_reshape_squeeze.3
  5.7 10.8 %all_gather.3 = s32[4,16,128,8]{2,3,1,0:T(8,128)S(1)} all-gather(s32[1,16,128,8]{2,3,1,0:T(8,128)S(1)} %copy.28), channel_id=1, replica_groups=mesh['dp'=1,'pp'=2,'ep'=4] {'ep'}, dimensions={0}, use_global_device_ids=true | all-gather | bytes 327680 | tf_op jit(solution)/shard_map/all_gather | solution.py:509
  16.5 0.6 gather_fusion
  17.1 0.0 copy-start.2
  17.1 0.7 copy-done.2
  17.8 2.4 convert_reduce_fusion
  20.3 0.2 reduce_window_sum.11
  20.5 0.1 copy.30
  20.5 0.1 copy.34
  20.6 0.1 copy.31
  20.7 0.0 copy-start.3
  20.7 0.1 copy.33
  20.8 0.5 copy-done.3
  21.3 0.1 copy.35
  21.4 0.6 subtract_select_fusion.tk_ref
  22.0 0.8 fusion.tri
  22.8 1.3 broadcast_in_dim.24.pos
  24.2 549.9 %decode_step.1 = (bf16[16,128,1024]{2,1,0:T(8,128)(2,1)}, bf16[16,128,8,64]{3,2,1,0:T(8,128)(2,1)}, bf16[16,128,8,64]{3,2,1,0:T(8,128)(2,1)}) custom-call(s32[16,15]{1,0:T(8,128)} %copy-done.3, s32[16,15]{1,0:T(8,128)} %subtract_select_fusion.tk_ref, bf16[16,128,1024]{2,1,0:T(8,128)(2,1)} %bitcast.37, s32[16,128,128]{2,1,0:T(8,128)} %broadcast_in_dim.24.pos, ...), custom_call_target="tpu_custom_call" | custom-call | flops 199999995904 | bytes 200000000 | tf_op jit(solution)/shard_map/decode_step/pallas_call | solution.py:422
  574.1 0.0 copy-start.1
  574.1 5.2 copy.41
  579.3 0.0 copy-done.1
  579.3 0.0 copy-start
  579.3 2.1 copy.42
  581.4 1.6 copy-done
  583.0 2.0 copy.43
  (13 shorter events, 0.2 us)
Async XLA Ops:
  17.1 0.7 copy-start.2
  20.7 0.6 copy-start.3
  574.1 5.2 copy-start.1
  579.3 3.7 copy-start

commit v3 on v2

--- a/solution.py
+++ b/solution.py
@@ -13,6 +13,8 @@
 BF16 = jnp.bfloat16
 TILE = 128
 GROUP = 16
+GROUP_UNROLL = 4
+TILE_UNROLL = 3
 PER_CHUNK = 4
 HIN_SLOTS = 4
 MESH = pl.DeviceIdType.MESH
@@ -49,35 +51,41 @@
     return jnp.concatenate(parts, axis=1)
 
 
-def dup_heads(vals):
+def spread(ref, vals):
+    tokens = vals.shape[0]
+    for g in range(8):
+        ref[pl.ds(g, tokens, stride=8), :] = vals[:, g * 128:(g + 1) * 128]
+
+
+def spread_heads(ref, vals):
+    tokens = vals.shape[0]
     low = lax.broadcasted_iota(jnp.int32, (1, 128), 1) < 64
-    parts = []
-    for j in range(vals.shape[1] // 128):
+    for j in range(4):
         block = vals[:, j * 128:(j + 1) * 128]
         other = pltpu.roll(block, 64, 1)
-        parts.append(jnp.where(low, block, other))
-        parts.append(jnp.where(low, other, block))
-    return jnp.concatenate(parts, axis=1)
+        ref[pl.ds(2 * j, tokens, stride=8), :] = jnp.where(low, block, other)
+        ref[pl.ds(2 * j + 1, tokens, stride=8), :] = jnp.where(low, other, block)
+
+
+def rows_of(ref, idx):
+    return ref[pl.ds(pl.multiple_of(idx * GROUP * 8, GROUP * 8), GROUP * 8), :].reshape(GROUP, 8, 128)
 
 
 def attn_project(hidden, pos, w, q3, k3, v3):
-    tokens = hidden.shape[0]
     normed = rms(hidden.astype(F32), w["a_gain"][...].astype(F32))
     cos_t = rope_table(pos, w["cos"])
     sin_t = rope_table(pos, w["sin"])
+    k = rope(dot(normed, w["k"][...]).astype(BF16).astype(F32), cos_t, sin_t)
+    spread_heads(k3, k.astype(BF16).astype(F32))
+    spread_heads(v3, dot(normed, w["v"][...]).astype(BF16).astype(F32))
     q = rope(dot(normed, w["q"][...]).astype(BF16).astype(F32), cos_t, sin_t)
-    q3[...] = q.astype(BF16).astype(F32).reshape(tokens, -1, 128)
-    k = rope(dot(normed, w["k"][...]).astype(BF16).astype(F32), cos_t, sin_t)
-    k3[...] = dup_heads(k.astype(BF16).astype(F32)).reshape(tokens, -1, 128)
-    v3[...] = dup_heads(dot(normed, w["v"][...]).astype(BF16).astype(F32)).reshape(tokens, -1, 128)
-
-
-def attn_group(idx, q3, k3, v3, o3, pos_ref, k_rows, v_rows):
-    base = pl.multiple_of(idx * GROUP, GROUP)
-    span = pl.ds(base, GROUP)
-    q = q3[span]
+    spread(q3, q.astype(BF16).astype(F32))
+
+
+def attn_scores(idx, q3, k3, k_rows):
+    q = rows_of(q3, idx)
     lane3 = lax.broadcasted_iota(jnp.int32, (1, 1, 128), 2)
-    prod = q * k3[span]
+    prod = q * rows_of(k3, idx)
     self_a = jnp.sum(jnp.where(lane3 < 64, prod, 0.0), axis=-1, keepdims=True)
     self_b = jnp.sum(jnp.where(lane3 < 64, 0.0, prod), axis=-1, keepdims=True)
     self_s = jnp.concatenate([self_a, self_b], axis=1) * 0.125
@@ -89,18 +97,24 @@
         both = dot_nt(q_rows[p * 32:(p + 1) * 32], keys)
         blocks.append(both[:16, :128].reshape(1, 16, 128))
         blocks.append(both[16:, 128:].reshape(1, 16, 128))
-    scores = jnp.concatenate(blocks, axis=0)
+    return jnp.concatenate(blocks, axis=0), self_s
+
+
+def attn_weights(idx, scores, self_s, pos_ref):
     row_i = lax.broadcasted_iota(jnp.int32, (16, 128), 0)
     lane_i = lax.broadcasted_iota(jnp.int32, (16, 128), 1)
     step = jnp.where((row_i % 8) == (lane_i % 8), lane_i // 8, 1000)
-    pos = pos_ref[span, :].reshape(GROUP, 1, 128)
+    pos = pos_ref[pl.ds(pl.multiple_of(idx * GROUP, GROUP), GROUP), :].reshape(GROUP, 1, 128)
     scores = jnp.where(step.reshape(1, 16, 128) < pos, scores * 0.125, -jnp.inf)
     top = jnp.maximum(jnp.max(scores, axis=-1, keepdims=True), self_s)
     weights = jnp.exp(scores - top)
     self_w = jnp.exp(self_s - top)
     inv = 1.0 / (jnp.sum(weights, axis=-1, keepdims=True) + self_w)
-    weights = (weights * inv).astype(BF16)
-    self_w = (self_w * inv).astype(BF16).astype(F32)
+    return (weights * inv).astype(BF16), (self_w * inv).astype(BF16).astype(F32)
+
+
+def attn_mix(idx, weights, self_w, v3, o3, v_rows):
+    row0 = idx * (GROUP * 128)
     zeros = jnp.zeros((16, 128), BF16)
     outs = []
     for p in range(GROUP // 2):
@@ -109,10 +123,10 @@
         lower = jnp.concatenate([zeros, weights[2 * p + 1]], axis=1)
         outs.append(dot(jnp.concatenate([upper, lower], axis=0), vals).reshape(2, 16, 64))
     out = jnp.concatenate(outs, axis=0)
-    v_new = v3[span][:, :, :64]
+    v_new = rows_of(v3, idx)[:, :, :64]
     out_a = out[:, :8] + self_w[:, :8] * v_new
     out_b = out[:, 8:] + self_w[:, 8:] * v_new
-    o3[span] = jnp.concatenate([out_a, out_b], axis=-1)
+    o3[pl.ds(pl.multiple_of(idx * GROUP * 8, GROUP * 8), GROUP * 8), :] = jnp.concatenate([out_a, out_b], axis=-1).reshape(GROUP * 8, 128)
 
 
 def moe_route(ids, normed, w_r, tri, rank_ref, gate_ref):
@@ -129,23 +143,34 @@
     gate_ref[...] = gates / jnp.sum(gates, axis=0, keepdims=True)
 
 
-def moe_tile(idx, expert, sub, first, normed, rank_ref, gate_ref, w, picks, terms):
+def moe_gather(j, slot, expert, sub, first, normed, rank_ref, gate_ref, picks, x_buf, g_buf):
     ranks = rank_ref[pl.ds(first + expert, 1), :]
     wanted = (lax.broadcasted_iota(jnp.int32, (TILE, 1), 0) + sub * TILE).astype(F32)
     picked = jnp.where(ranks == wanted, 1.0, 0.0)
     gate = jnp.sum(picked * gate_ref[pl.ds(first + expert, 1), :], axis=-1, keepdims=True)
-    at = pl.ds(pl.multiple_of(idx * TILE, TILE), TILE)
-    picks[:, at] = picked.T.astype(BF16)
-    rows = dot(picked.astype(BF16), normed[...]).astype(BF16)
-    act = jax.nn.silu(dot(rows, w["gate"][expert])) * dot(rows, w["up"][expert])
-    terms[at, :] = (gate * dot(act.astype(BF16), w["down"][expert])).astype(BF16)
+    g_buf[slot] = jnp.broadcast_to(gate, (TILE, 128))
+    picks[:, pl.ds(pl.multiple_of(j * TILE, TILE), TILE)] = picked.T.astype(BF16)
+    x_buf[slot] = dot(picked.astype(BF16), normed[...]).astype(BF16)
+
+
+def moe_expand(slot, expert, w, x_buf, a_buf):
+    rows = x_buf[slot]
+    a_buf[slot] = (jax.nn.silu(dot(rows, w["gate"][expert])) * dot(rows, w["up"][expert])).astype(BF16)
+
+
+def moe_contract(j, slot, expert, w, a_buf, g_buf, terms):
+    y = dot(a_buf[slot], w["down"][expert])
+    gate = g_buf[slot]
+    at = pl.ds(pl.multiple_of(j * TILE, TILE), TILE)
+    for p in range(8):
+        terms[at, p * 128:(p + 1) * 128] = (gate * y[:, p * 128:(p + 1) * 128]).astype(BF16)
 
 
 def step_kernel(
     tile_count,
     te_ref, tk_ref, hid, pos, k_cache, v_cache, ids, wq_h, wk_h, wv_h, wo_h, a_gain, m_gain, f_gain, cos_ref, sin_ref, w_r, wg_h, wu_h, wd_h, tri,
     out, kn_out, vn_out,
-    n_buf, hin, mid, ho, k_buf, v_buf, wq, wk, wv, wo, wg, wu, wd, part, own, xsum, rb1, rb2, picks, terms, q3, k3, v3, o3, kn, vn, rank_ref, gate_ref,
+    n_buf, hin, mid, ho, k_buf, v_buf, wq, wk, wv, wo, wg, wu, wd, part, own, xsum, rb1, rb2, picks, terms, x_buf, a_buf, g_buf, q3, k3, v3, o3, kn, vn, rank_ref, gate_ref,
     w_sem, hin_sem, kv_sem, new_sem, dx_send, dx_recv, dc_send, dc_recv, dr_send, dr_recv, r1_send, r1_recv, r2_send, r2_recv, hop_send, out_loc, out_recv, credit,
 ):
     chunks, tokens = hid.shape[0], hid.shape[1]
@@ -215,17 +240,15 @@
         s = lax.rem(c, 2)
         return pltpu.make_async_copy(ho.at[s], out.at[c], out_loc.at[s])
 
-    for copy in weight_copies[:3]:
-        copy.start()
-
     @pl.when(pp == 0)
     def _():
         hin_copy(0).start()
 
+    for copy in weight_copies[:3]:
+        copy.start()
     for copy in kv_copies(0):
         copy.start()
-    for copy in weight_copies[3:]:
-        copy.start()
+    weight_copies[3].start()
 
     @pl.when(pp == 0)
     def _():
@@ -251,8 +274,8 @@
                 copy.wait()
 
         attn_project(hin[lax.rem(c, HIN_SLOTS)], pos[c], w, q3, k3, v3)
-        kn[...] = k3[...][:, :, :64].astype(BF16)
-        vn[...] = v3[...][:, :, :64].astype(BF16)
+        kn[...] = k3[...].reshape(tokens, 8, 128)[:, :, :64].astype(BF16)
+        vn[...] = v3[...].reshape(tokens, 8, 128)[:, :, :64].astype(BF16)
         for copy in new_copies(c):
             copy.start()
 
@@ -276,11 +299,22 @@
         for copy in kv_copies(c):
             copy.wait()
 
+        @pl.when(c == 0)
+        def _():
+            for copy in weight_copies[4:]:
+                copy.start()
+
         def body(idx, carry):
-            attn_group(idx, q3, k3, v3, o3, pos.at[c], k_buf, v_buf)
+            base = idx * GROUP_UNROLL
+            ahead = attn_scores(base, q3, k3, k_buf)
+            for u in range(GROUP_UNROLL):
+                scores = ahead
+                if u + 1 < GROUP_UNROLL:
+                    ahead = attn_scores(base + u + 1, q3, k3, k_buf)
+                attn_mix(base + u, *attn_weights(base + u, *scores, pos.at[c]), v3, o3, v_buf)
             return carry
 
-        lax.fori_loop(0, tokens // GROUP, body, 0)
+        lax.fori_loop(0, tokens // (GROUP * GROUP_UNROLL), body, 0)
 
         @pl.when(c + 1 < chunks)
         def _():
@@ -292,7 +326,7 @@
             weight_copies[3].wait()
 
         hidden = hin[lax.rem(c, HIN_SLOTS)].astype(F32)
-        attn_out = o3[...].reshape(tokens, 1024).astype(BF16)
+        attn_out = jnp.concatenate([o3[pl.ds(g, tokens, stride=8), :].astype(BF16) for g in range(8)], axis=1)
         new_mid = (hidden + dot(attn_out, wo[...])).astype(BF16)
         mid[lax.rem(c, 3)] = new_mid
         n_buf[lax.rem(c, 3), pl.ds(0, tokens), :] = rms(new_mid.astype(F32), m_gain[...].astype(F32))
@@ -316,20 +350,38 @@
             for copy in weight_copies[4:]:
                 copy.wait()
 
+        def gather(j, slot):
+            moe_gather(j, slot, te_ref[c, j], tk_ref[c, j], first, normed, rank_ref, gate_ref, picks, x_buf, g_buf)
+
+        def expand(j, slot):
+            moe_expand(slot, te_ref[c, j], w, x_buf, a_buf)
+
+        def contract(j, slot):
+            moe_contract(j, slot, te_ref[c, j], w, a_buf, g_buf, terms)
+
+        last = tile_count // TILE_UNROLL
+
         def body(idx, carry):
-            moe_tile(idx, te_ref[c, idx], tk_ref[c, idx], first, normed, rank_ref, gate_ref, w, picks, terms)
+            base = idx * TILE_UNROLL
+            expand(base, 0)
+            gather(base + 1, 1)
+            for u in range(1, TILE_UNROLL):
+                expand(base + u, u)
+                if u + 1 < TILE_UNROLL:
+                    gather(base + u + 1, u + 1)
+                else:
+                    gather(lax.rem(base + TILE_UNROLL, tile_count), 0)
+                contract(base + u - 1, u - 1)
+            contract(base + TILE_UNROLL - 1, TILE_UNROLL - 1)
             return carry
 
-        lax.fori_loop(0, tile_count, body, 0)
-
-        def combine(idx, carry):
-            cols = pl.ds(pl.multiple_of(idx * 256, 256), 256)
-            part[:, cols] = dot(picks[...], terms[:, cols])
-            return carry
-
-        lax.fori_loop(0, 4, combine, 0)
+        gather(0, 0)
+        lax.fori_loop(0, last, body, 0)
+        half = 2 * tokens
+        part[pl.ds(half, half), :] = dot(picks[pl.ds(half, half), :], terms[...])
         relayed.wait_send()
         r1_copy(c).start()
+        part[pl.ds(0, half), :] = dot(picks[pl.ds(0, half), :], terms[...])
 
     def finish(c):
         s = lax.rem(c, 2)
@@ -449,10 +501,13 @@
             pltpu.VMEM((3, tokens, 1024), F32),
             pltpu.VMEM((wide, tile_count * TILE), BF16),
             pltpu.VMEM((tile_count * TILE, 1024), BF16),
-            pltpu.VMEM((tokens, 8, 128), F32),
-            pltpu.VMEM((tokens, 8, 128), F32),
-            pltpu.VMEM((tokens, 8, 128), F32),
-            pltpu.VMEM((tokens, 8, 128), F32),
+            pltpu.VMEM((TILE_UNROLL, TILE, 1024), BF16),
+            pltpu.VMEM((TILE_UNROLL, TILE, 512), BF16),
+            pltpu.VMEM((TILE_UNROLL, TILE, 128), F32),
+            pltpu.VMEM((tokens * 8, 128), F32),
+            pltpu.VMEM((tokens * 8, 128), F32),
+            pltpu.VMEM((tokens * 8, 128), F32),
+            pltpu.VMEM((tokens * 8, 128), F32),
             pltpu.VMEM((tokens, 8, 64), BF16),
             pltpu.VMEM((tokens, 8, 64), BF16),
             pltpu.VMEM((32, wide), F32),

time: 585 us -> 452 us (0.77)
  Pallas kernels: 550 us -> 417 us
    pallas_call x1, Pallas kernels: 550 us -> 417 us  [step_call(): pl.pallas_call(functools.partial(step_kernel, tile_count), out_shape=(jax...]
where the time goes in v3:
time: 452 us
  Pallas kernels  417 us (92%)
  local copies, waits for them, and re-layouts  19 us (4%)
  blocking collectives  10.8 us (2%)
    pallas_call x1, Pallas kernels, step_call(): pl.pallas_call(functools.partial(step_kernel, tile_count), out_shape=(jax...  417 us
    unnamed x13, local copies, waits for them, and re-layouts  13.9 us
    all_gather x1, blocking collectives, device_fn(): lax.all_gather(expert_ids[0].reshape(chunks, tokens, 8), 'ep', axis=0, ti...  10.8 us

profile of v3, /device:TPU:0, one launch (start us, length us, event | category | flops | bytes accessed | tf_op | source)
XLA Modules:
  0.0 452.1 jit_solution(4840714363944817330)
XLA Ops:
  0.7 0.1 fusion.4
  0.8 1.3 reshape.274.f_gain
  2.1 0.1 fusion.3
  2.2 0.1 pad_maximum_fusion
  2.3 0.7 tile.21.sin_ref
  3.0 0.7 tile.9.cos_ref
  3.6 0.8 copy.36
  4.4 0.1 broadcast_in_dim.23
  4.5 1.0 copy.27
  5.5 0.1 all_gather_reshape_squeeze.3
  5.7 10.8 %all_gather.3 = s32[4,16,128,8]{2,3,1,0:T(8,128)S(1)} all-gather(s32[1,16,128,8]{2,3,1,0:T(8,128)S(1)} %copy.28), channel_id=1, replica_groups=mesh['dp'=1,'pp'=2,'ep'=4] {'ep'}, dimensions={0}, use_global_device_ids=true | all-gather | bytes 327680 | tf_op jit(solution)/shard_map/all_gather | solution.py:564
  16.5 0.6 gather_fusion
  17.1 0.0 copy-start.2
  17.1 0.7 copy-done.2
  17.8 2.4 convert_reduce_fusion
  20.3 0.2 reduce_window_sum.11
  20.5 0.1 copy.30
  20.5 0.1 copy.34
  20.6 0.1 copy.31
  20.7 0.0 copy-start.3
  20.7 0.1 copy.33
  20.8 0.5 copy-done.3
  21.3 0.1 copy.35
  21.4 0.6 subtract_select_fusion.tk_ref
  22.0 0.8 fusion.tri
  22.8 1.3 broadcast_in_dim.24.pos
  24.2 417.0 %decode_step.1 = (bf16[16,128,1024]{2,1,0:T(8,128)(2,1)}, bf16[16,128,8,64]{3,2,1,0:T(8,128)(2,1)}, bf16[16,128,8,64]{3,2,1,0:T(8,128)(2,1)}) custom-call(s32[16,15]{1,0:T(8,128)} %copy-done.3, s32[16,15]{1,0:T(8,128)} %subtract_select_fusion.tk_ref, bf16[16,128,1024]{2,1,0:T(8,128)(2,1)} %bitcast.37, s32[16,128,128]{2,1,0:T(8,128)} %broadcast_in_dim.24.pos, ...), custom_call_target="tpu_custom_call" | custom-call | flops 199999995904 | bytes 200000000 | tf_op jit(solution)/shard_map/decode_step/pallas_call | solution.py:474
  441.2 0.0 copy-start.1
  441.2 5.2 %copy.41 = bf16[64,32,1024]{2,1,0:T(8,128)(2,1)} copy(bf16[64,32,1024]{2,1,0:T(8,128)(2,1)} %bitcast.33) | data formatting | bytes 8388608
  446.4 0.0 copy-done.1
  446.4 0.0 copy-start
  446.4 2.1 copy.42
  448.5 1.6 copy-done
  450.1 2.0 copy.43
  (13 shorter events, 0.2 us)
Async XLA Ops:
  17.1 0.7 copy-start.2
  20.7 0.6 copy-start.3
  441.2 5.2 %copy-start.1 = (bf16[16,128,8,64]{3,2,1,0:T(8,128)(2,1)S(1)}, bf16[16,128,8,64]{3,2,1,0:T(8,128)(2,1)}, u32[]{:S(2)}) copy-start(bf16[16,128,8,64]{3,2,1,0:T(8,128)(2,1)} %get-tuple-element.7) | copy-start | bytes 6291460
  446.4 3.7 copy-start

commit v4 on v3

--- a/solution.py
+++ b/solution.py
@@ -2,6 +2,7 @@
 
 import jax
 import jax.numpy as jnp
+import numpy as np
 from jax import lax
 from jax.experimental import pallas as pl
 from jax.experimental.pallas import tpu as pltpu
@@ -17,6 +18,7 @@
 TILE_UNROLL = 3
 PER_CHUNK = 4
 HIN_SLOTS = 4
+PIECES = 4
 MESH = pl.DeviceIdType.MESH
 
 
@@ -36,7 +38,7 @@
 def rope_table(pos, table_ref):
     picked = jnp.zeros(pos.shape, F32)
     for t in range(table_ref.shape[0]):
-        picked = jnp.where(pos == t + 1, table_ref[t:t + 1, :], picked)
+        picked = jnp.where(pos == float(t + 1), table_ref[t:t + 1, :], picked)
     return picked
 
 
@@ -103,7 +105,7 @@
 def attn_weights(idx, scores, self_s, pos_ref):
     row_i = lax.broadcasted_iota(jnp.int32, (16, 128), 0)
     lane_i = lax.broadcasted_iota(jnp.int32, (16, 128), 1)
-    step = jnp.where((row_i % 8) == (lane_i % 8), lane_i // 8, 1000)
+    step = jnp.where((row_i % 8) == (lane_i % 8), lane_i // 8, 1000).astype(F32)
     pos = pos_ref[pl.ds(pl.multiple_of(idx * GROUP, GROUP), GROUP), :].reshape(GROUP, 1, 128)
     scores = jnp.where(step.reshape(1, 16, 128) < pos, scores * 0.125, -jnp.inf)
     top = jnp.maximum(jnp.max(scores, axis=-1, keepdims=True), self_s)
@@ -129,17 +131,37 @@
     o3[pl.ds(pl.multiple_of(idx * GROUP * 8, GROUP * 8), GROUP * 8), :] = jnp.concatenate([out_a, out_b], axis=-1).reshape(GROUP * 8, 128)
 
 
-def moe_route(ids, normed, w_r, tri, rank_ref, gate_ref):
+def plan_tiles(ids, first, tri, member_ref, rank_ref, table_ref):
     tokens = ids.shape[1]
     expert_i = lax.broadcasted_iota(jnp.int32, (32, tokens), 0)
     chosen = jnp.zeros((32, tokens), F32)
     for s in range(ids.shape[0]):
         chosen = jnp.where(ids[s:s + 1, :] == expert_i, 1.0, chosen)
+    member_ref[...] = chosen
     rank = dot(chosen.astype(BF16), tri[...])
     rank_ref[...] = jnp.where(chosen > 0.0, rank, -1.0)
+    local = member_ref[pl.ds(pl.multiple_of(first, 8), 8), :]
+    counts = jnp.sum(local, axis=-1, keepdims=True).astype(jnp.int32)
+    tiles = jnp.broadcast_to(lax.shift_right_logical(counts + (TILE - 1), 7), (8, 128))
+    lane = lax.broadcasted_iota(jnp.int32, (1, 128), 1)
+    end = jnp.zeros((1, 128), jnp.int32)
+    start = jnp.zeros((1, 128), jnp.int32)
+    expert = jnp.zeros((1, 128), jnp.int32)
+    for e in range(8):
+        end = end + tiles[e:e + 1, :]
+        passed = lane >= end
+        expert = jnp.where(passed, expert + 1, expert)
+        start = jnp.where(passed, end, start)
+    sub = jnp.where(expert < 8, lane - start, 1000)
+    table_ref[0:1, :] = jnp.minimum(expert, 7)
+    table_ref[1:2, :] = sub
+
+
+def moe_gates(normed, w_r, rank_ref, gate_ref):
+    chosen = rank_ref[...] >= 0.0
     logits = dot_nt(w_r[...], normed)
-    top = jnp.max(jnp.where(chosen > 0.0, logits, -jnp.inf), axis=0, keepdims=True)
-    gates = jnp.where(chosen > 0.0, jnp.exp(logits - top), 0.0)
+    top = jnp.max(jnp.where(chosen, logits, -jnp.inf), axis=0, keepdims=True)
+    gates = jnp.where(chosen, jnp.exp(logits - top), 0.0)
     gate_ref[...] = gates / jnp.sum(gates, axis=0, keepdims=True)
 
 
@@ -168,10 +190,10 @@
 
 def step_kernel(
     tile_count,
-    te_ref, tk_ref, hid, pos, k_cache, v_cache, ids, wq_h, wk_h, wv_h, wo_h, a_gain, m_gain, f_gain, cos_ref, sin_ref, w_r, wg_h, wu_h, wd_h, tri,
+    hid, seq, k_cache, v_cache, ids_own, wq_h, wk_h, wv_h, wo_h, a_gain, m_gain, f_gain, cos_ref, sin_ref, w_r, wg_h, wu_h, wd_h, tri,
     out, kn_out, vn_out,
-    n_buf, hin, mid, ho, k_buf, v_buf, wq, wk, wv, wo, wg, wu, wd, part, own, xsum, rb1, rb2, picks, terms, x_buf, a_buf, g_buf, q3, k3, v3, o3, kn, vn, rank_ref, gate_ref,
-    w_sem, hin_sem, kv_sem, new_sem, dx_send, dx_recv, dc_send, dc_recv, dr_send, dr_recv, r1_send, r1_recv, r2_send, r2_recv, hop_send, out_loc, out_recv, credit,
+    n_buf, hin, mid, ho, k_buf, v_buf, wq, wk, wv, wo, wg, wu, wd, part, own, xsum, rb1, rb2, picks, terms, x_buf, a_buf, g_buf, q3, k3, v3, o3, kn, vn, rank_buf, gate_ref, member, pos, ids, table, smem_table,
+    w_sem, ids_send, ids_recv, table_sem, hin_sem, kv_sem, new_sem, dx_send, dx_recv, dc_send, dc_recv, dr_send, dr_recv, r1_send, r1_recv, r2_send, r2_recv, hop_send, out_loc, out_recv, credit,
 ):
     chunks, tokens = hid.shape[0], hid.shape[1]
     gathered = 4 * tokens
@@ -183,17 +205,20 @@
     beside = (dp, pp, ep + 1 - 2 * lax.rem(ep, 2))
     first = ep * 8
 
+    diagonal = (dp, pp, lax.rem(ep + 3 - 2 * lax.rem(ep, 2), 4))
+
     barrier = pltpu.get_barrier_semaphore()
-    for peer in (other_pp, across, beside):
+    for peer in (other_pp, across, beside, diagonal):
         pl.semaphore_signal(barrier, inc=1, device_id=peer, device_id_type=MESH)
-    pl.semaphore_wait(barrier, 3)
+    pl.semaphore_wait(barrier, 4)
 
     attn_w = [(wq_h, wq), (wk_h, wk), (wv_h, wv), (wo_h, wo)]
     moe_w = [(wg_h, wg), (wu_h, wu), (wd_h, wd)]
     weight_copies = [pltpu.make_async_copy(s, d, w_sem.at[j]) for j, (s, d) in enumerate(attn_w + moe_w)]
 
-    def hin_copy(c):
-        return pltpu.make_async_copy(hid.at[c], hin.at[lax.rem(c, HIN_SLOTS)], hin_sem.at[lax.rem(c, HIN_SLOTS)])
+    def hin_copies(c):
+        h = lax.rem(c, HIN_SLOTS)
+        return [pltpu.make_async_copy(hid.at[c, piece(p)], hin.at[h, piece(p)], hin_sem.at[h, p]) for p in range(PIECES)]
 
     def kv_copies(c):
         return (pltpu.make_async_copy(k_cache.at[c], k_buf, kv_sem.at[0]), pltpu.make_async_copy(v_cache.at[c], v_buf, kv_sem.at[1]))
@@ -223,26 +248,42 @@
         s = lax.rem(c, 2)
         return remote(part.at[pl.ds(2 * tokens, 2 * tokens)], rb1.at[s], r1_send.at[s], r1_recv.at[s], beside)
 
-    def r2_copy(c):
+    rows = tokens // PIECES
+
+    def piece(p):
+        return pl.ds(p * rows, rows)
+
+    def r2_copy(c, p):
         s = lax.rem(c, 3)
-        return remote(xsum, rb2.at[s], r2_send.at[s], r2_recv.at[s], across)
-
-    def hop_copy(c):
+        return remote(xsum.at[piece(p)], rb2.at[s, piece(p)], r2_send.at[s, p], r2_recv.at[s, p], across)
+
+    def hop_copy(c, p):
         s = lax.rem(c, 2)
         h = lax.rem(c, HIN_SLOTS)
-        return remote(ho.at[s], hin.at[h], hop_send.at[s], hin_sem.at[h], other_pp)
-
-    def out_copy(c):
+        return remote(ho.at[s, piece(p)], hin.at[h, piece(p)], hop_send.at[s, p], hin_sem.at[h, p], other_pp)
+
+    def out_copy(c, p):
         s = lax.rem(c, 2)
-        return remote(ho.at[s], out.at[c], hop_send.at[s], out_recv.at[c], other_pp)
-
-    def out_local(c):
+        return remote(ho.at[s, piece(p)], out.at[c, piece(p)], hop_send.at[s, p], out_recv.at[c, p], other_pp)
+
+    def out_local(c, p):
         s = lax.rem(c, 2)
-        return pltpu.make_async_copy(ho.at[s], out.at[c], out_loc.at[s])
+        return pltpu.make_async_copy(ho.at[s, piece(p)], out.at[c, piece(p)], out_loc.at[s, p])
+
+    def ids_copies():
+        return [remote(ids_own, ids.at[j], ids_send.at[j], ids_recv.at[j], peer) for j, peer in ((1, across), (2, beside), (3, diagonal))]
+
+    def table_copy(c):
+        s = lax.rem(c, 2)
+        return pltpu.make_async_copy(table, smem_table.at[s], table_sem)
+
+    for copy in ids_copies():
+        copy.start()
 
     @pl.when(pp == 0)
     def _():
-        hin_copy(0).start()
+        for copy in hin_copies(0):
+            copy.start()
 
     for copy in weight_copies[:3]:
         copy.start()
@@ -252,12 +293,26 @@
 
     @pl.when(pp == 0)
     def _():
-        hin_copy(1).start()
+        for copy in hin_copies(1):
+            copy.start()
 
     w = {"a_gain": a_gain, "cos": cos_ref, "sin": sin_ref, "q": wq, "k": wk, "v": wv, "gate": wg, "up": wu, "down": wd}
 
+    def plan(c):
+        @pl.when(c == 0)
+        def _():
+            ids[0] = ids_own[...]
+            for copy in ids_copies():
+                copy.wait()
+
+        chosen_ids = jnp.concatenate([ids[j, c] for j in range(4)], axis=1)
+        plan_tiles(chosen_ids, first, tri, member, rank_buf.at[lax.rem(c, 2)], table)
+        table_copy(c).start()
+
     def project(c):
-        hin_copy(c).wait()
+        plan(c)
+        for copy in hin_copies(c):
+            copy.wait()
 
         @pl.when(c == 0)
         def _():
@@ -266,14 +321,17 @@
 
         @pl.when(jnp.logical_and(pp == 0, c + 2 < chunks))
         def _():
-            hin_copy(c + 2).start()
+            for copy in hin_copies(c + 2):
+                copy.start()
 
         @pl.when(c > 0)
         def _():
             for copy in new_copies(c - 1):
                 copy.wait()
 
-        attn_project(hin[lax.rem(c, HIN_SLOTS)], pos[c], w, q3, k3, v3)
+        seq_row = seq[pl.ds(c, 1), :].astype(F32)
+        pos[...] = jnp.broadcast_to(seq_row, (128, 128)).T
+        attn_project(hin[lax.rem(c, HIN_SLOTS)], pos[...], w, q3, k3, v3)
         kn[...] = k3[...].reshape(tokens, 8, 128)[:, :, :64].astype(BF16)
         vn[...] = v3[...].reshape(tokens, 8, 128)[:, :, :64].astype(BF16)
         for copy in new_copies(c):
@@ -285,7 +343,8 @@
         copy.wait_recv()
         s = lax.rem(c, 2)
         xsum[...] = part[pl.ds(tokens, tokens), :] + rb1[s, pl.ds(tokens, tokens), :]
-        r2_copy(c).start()
+        for p in range(PIECES):
+            r2_copy(c, p).start()
         own[...] = part[pl.ds(0, tokens), :] + rb1[s, pl.ds(0, tokens), :]
 
     def relay(c):
@@ -296,6 +355,7 @@
         dc_copy(c).wait_send()
 
     def attend(c):
+        table_copy(c).wait()
         for copy in kv_copies(c):
             copy.wait()
 
@@ -311,7 +371,7 @@
                 scores = ahead
                 if u + 1 < GROUP_UNROLL:
                     ahead = attn_scores(base + u + 1, q3, k3, k_buf)
-                attn_mix(base + u, *attn_weights(base + u, *scores, pos.at[c]), v3, o3, v_buf)
+                attn_mix(base + u, *attn_weights(base + u, *scores, pos), v3, o3, v_buf)
             return carry
 
         lax.fori_loop(0, tokens // (GROUP * GROUP_UNROLL), body, 0)
@@ -343,7 +403,9 @@
         relayed = dr_copy(c)
         relayed.wait_recv()
         normed = n_buf.at[s]
-        moe_route(ids[c], normed[...], w_r, tri, rank_ref, gate_ref)
+        rank_ref = rank_buf.at[lax.rem(c, 2)]
+        tile_ref = smem_table.at[lax.rem(c, 2)]
+        moe_gates(normed[...], w_r, rank_ref, gate_ref)
 
         @pl.when(c == 0)
         def _():
@@ -351,13 +413,13 @@
                 copy.wait()
 
         def gather(j, slot):
-            moe_gather(j, slot, te_ref[c, j], tk_ref[c, j], first, normed, rank_ref, gate_ref, picks, x_buf, g_buf)
+            moe_gather(j, slot, tile_ref[0, j], tile_ref[1, j], first, normed, rank_ref, gate_ref, picks, x_buf, g_buf)
 
         def expand(j, slot):
-            moe_expand(slot, te_ref[c, j], w, x_buf, a_buf)
+            moe_expand(slot, tile_ref[0, j], w, x_buf, a_buf)
 
         def contract(j, slot):
-            moe_contract(j, slot, te_ref[c, j], w, a_buf, g_buf, terms)
+            moe_contract(j, slot, tile_ref[0, j], w, a_buf, g_buf, terms)
 
         last = tile_count // TILE_UNROLL
 
@@ -385,35 +447,45 @@
 
     def finish(c):
         s = lax.rem(c, 2)
-        copy = r2_copy(c)
-        copy.wait_recv()
-        copy.wait_send()
-        mixed = (own[...] + rb2[lax.rem(c, 3)]).astype(BF16)
-        result = (mid[lax.rem(c, 3)].astype(F32) + mixed.astype(F32)).astype(BF16)
-
-        @pl.when(pp == 0)
-        def _():
-            @pl.when(c >= 2)
+
+        @pl.when(jnp.logical_and(pp == 0, c >= HIN_SLOTS))
+        def _():
+            pl.semaphore_wait(credit, 1)
+
+        @pl.when(c >= 2)
+        def _():
+            for p in range(PIECES):
+                @pl.when(pp == 0)
+                def _():
+                    hop_copy(c - 2, p).wait_send()
+
+                @pl.when(pp == 1)
+                def _():
+                    out_copy(c - 2, p).wait_send()
+                    out_local(c - 2, p).wait()
+
+        for p in range(PIECES):
+            r2_copy(c, p).wait_recv()
+            at = piece(p)
+            mixed = (own[at, :] + rb2[lax.rem(c, 3), at, :]).astype(BF16)
+            result = (mid[lax.rem(c, 3), at, :].astype(F32) + mixed.astype(F32)).astype(BF16)
+
+            @pl.when(pp == 0)
             def _():
-                hop_copy(c - 2).wait_send()
-
-            @pl.when(c >= HIN_SLOTS)
+                ho[s, at, :] = result
+                hop_copy(c, p).start()
+
+            @pl.when(pp == 1)
             def _():
-                pl.semaphore_wait(credit, 1)
-
-            ho[s] = result
-            hop_copy(c).start()
-
-        @pl.when(pp == 1)
-        def _():
-            @pl.when(c >= 2)
-            def _():
-                out_copy(c - 2).wait_send()
-                out_local(c - 2).wait()
-
-            ho[s] = rms(result.astype(F32), f_gain[...].astype(F32))
-            out_copy(c).start()
-            out_local(c).start()
+                vals = result.astype(F32)
+                vals = vals * lax.rsqrt(jnp.mean(vals * vals, axis=-1, keepdims=True) + EPS)
+                for g in range(8):
+                    ho[s, at, g * 128:(g + 1) * 128] = (vals[:, g * 128:(g + 1) * 128] * f_gain[g:g + 1, :]).astype(BF16)
+                out_copy(c, p).start()
+                out_local(c, p).start()
+
+        for p in range(PIECES):
+            r2_copy(c, p).wait_send()
 
     def step(i, carry):
         @pl.when(i < chunks)
@@ -450,10 +522,12 @@
     @pl.when(pp == 0)
     def _():
         for c in (chunks - 2, chunks - 1):
-            hop_copy(c).wait_send()
+            for p in range(PIECES):
+                hop_copy(c, p).wait_send()
 
         def arrived(c, carry):
-            out_copy(c).wait_recv()
+            for p in range(PIECES):
+                out_copy(c, p).wait_recv()
             return carry
 
         lax.fori_loop(0, chunks, arrived, 0)
@@ -461,13 +535,13 @@
     @pl.when(pp == 1)
     def _():
         for c in (chunks - 2, chunks - 1):
-            out_copy(c).wait_send()
-            out_local(c).wait()
+            for p in range(PIECES):
+                out_copy(c, p).wait_send()
+                out_local(c, p).wait()
 
 
 def step_call(args, chunks, tokens, tile_count):
     vmem = pl.BlockSpec(memory_space=pltpu.VMEM)
-    smem = pl.BlockSpec(memory_space=pltpu.SMEM)
     hbm = pl.BlockSpec(memory_space=pl.ANY)
     wide = 4 * tokens
     dma = pltpu.SemaphoreType.DMA
@@ -478,7 +552,7 @@
             jax.ShapeDtypeStruct((chunks, tokens, 8, 64), BF16),
             jax.ShapeDtypeStruct((chunks, tokens, 8, 64), BF16),
         ),
-        in_specs=[smem, smem, hbm, vmem, hbm, hbm, vmem, hbm, hbm, hbm, hbm, vmem, vmem, vmem, vmem, vmem, vmem, hbm, hbm, hbm, vmem],
+        in_specs=[hbm, vmem, hbm, hbm, vmem, hbm, hbm, hbm, hbm, vmem, vmem, vmem, vmem, vmem, vmem, hbm, hbm, hbm, vmem],
         out_specs=(hbm, hbm, hbm),
         scratch_shapes=[
             pltpu.VMEM((3, wide, 1024), BF16),
@@ -510,32 +584,23 @@
             pltpu.VMEM((tokens * 8, 128), F32),
             pltpu.VMEM((tokens, 8, 64), BF16),
             pltpu.VMEM((tokens, 8, 64), BF16),
+            pltpu.VMEM((2, 32, wide), F32),
             pltpu.VMEM((32, wide), F32),
             pltpu.VMEM((32, wide), F32),
-            dma((7,)), dma((HIN_SLOTS,)), dma((2,)), dma((2,)),
+            pltpu.VMEM((tokens, 128), F32),
+            pltpu.VMEM((4, chunks, 8, tokens), jnp.int32),
+            pltpu.VMEM((8, 128), jnp.int32),
+            pltpu.SMEM((2, 8, 128), jnp.int32),
+            dma((7,)), dma((4,)), dma((4,)), dma(()), dma((HIN_SLOTS, PIECES)), dma((2,)), dma((2,)),
             dma((3,)), dma((3,)), dma((3,)), dma((3,)), dma((3,)), dma((3,)),
-            dma((2,)), dma((2,)), dma((3,)), dma((3,)),
-            dma((2,)), dma((2,)), dma((chunks,)),
+            dma((2,)), dma((2,)), dma((3, PIECES)), dma((3, PIECES)),
+            dma((2, PIECES)), dma((2, PIECES)), dma((chunks, PIECES)),
             pltpu.SemaphoreType.REGULAR,
         ],
         compiler_params=pltpu.CompilerParams(collective_id=0, has_side_effects=True, vmem_limit_bytes=67043328),
         name="decode_step",
         cost_estimate=pl.CostEstimate(flops=2 * 10**11, bytes_accessed=2 * 10**8, transcendentals=0),
     )(*args)
-
-
-def tile_tables(ids, first, tile_count):
-    local = first + jnp.arange(8, dtype=jnp.int32)
-    counts = jnp.sum((ids[:, None] == local[None, :, None, None]).astype(jnp.int32), axis=(2, 3))
-    tiles = (counts + TILE - 1) // TILE
-    ends = jnp.cumsum(tiles, axis=1)
-    idx = jnp.arange(tile_count, dtype=jnp.int32)
-    expert = jnp.sum((idx[None, :, None] >= ends[:, None, :]).astype(jnp.int32), axis=-1)
-    safe = jnp.minimum(expert, 7)
-    starts = ends - tiles
-    start = jnp.sum(jnp.where(safe[:, :, None] == jnp.arange(8)[None, None, :], starts[:, None, :], 0), axis=-1)
-    sub = jnp.where(expert < 8, idx[None, :] - start, 1000)
-    return safe, sub.astype(jnp.int32)
 
 
 def solution(mesh):
@@ -549,26 +614,19 @@
     out_specs = (P(None, rows_spec, None), new_spec, new_spec)
 
     def device_fn(hidden_in, seq_pos, k_cache, v_cache, expert_ids, w_query, w_key, w_value, w_out, attn_gain, mlp_gain, w_router, w_gate, w_up, w_down, final_gain):
-        ep_idx = lax.axis_index("ep")
         micro, rows = seq_pos.shape
         chunks = micro // PER_CHUNK
         tokens = PER_CHUNK * rows
         wide = 4 * tokens
         tile_count = (wide * 2 - 8) // TILE + 8
-        pos = jnp.broadcast_to(seq_pos.reshape(micro * rows, 1), (micro * rows, 128)).reshape(chunks, tokens, 128)
-        angles = jnp.arange(1, 17, dtype=F32)[:, None] * THETA ** (-jnp.arange(32, dtype=F32) / 32)
-        cos_t = jnp.tile(jnp.cos(angles), (1, 4))
-        sin_t = jnp.tile(jnp.concatenate([-jnp.sin(angles), jnp.sin(angles)], axis=1), (1, 2))
-        beside = ep_idx + 1 - 2 * (ep_idx % 2)
-        order = jnp.stack([ep_idx, (ep_idx + 2) % 4, beside, (beside + 2) % 4])
-        ids = lax.all_gather(expert_ids[0].reshape(chunks, tokens, 8), "ep", axis=0, tiled=False)
-        ids = jnp.transpose(ids[order], (1, 3, 0, 2)).reshape(chunks, 8, wide)
-        te, tk = tile_tables(ids, ep_idx * 8, tile_count)
-        ti = jnp.arange(wide)
-        tri = (ti[:, None] < ti[None, :]).astype(BF16)
+        angles = np.arange(1, 17)[:, None] * THETA ** (-np.arange(32) / 32)
+        cos_t = jnp.asarray(np.tile(np.cos(angles), (1, 4)), F32)
+        sin_t = jnp.asarray(np.tile(np.concatenate([-np.sin(angles), np.sin(angles)], axis=1), (1, 2)), F32)
+        tri = jnp.asarray(np.triu(np.ones((wide, wide)), 1), BF16)
+        ids = jnp.swapaxes(expert_ids[0].reshape(chunks, tokens, 8), 1, 2)
         args = (
-            te, tk, hidden_in.reshape(chunks, tokens, 1024), pos, k_cache.reshape(chunks, tokens * 128, 64), v_cache.reshape(chunks, tokens * 128, 64),
-            ids, w_query[0], w_key[0], w_value[0], w_out[0], attn_gain, mlp_gain, final_gain.reshape(1, -1), cos_t, sin_t, w_router[0].T,
+            hidden_in.reshape(chunks, tokens, 1024), seq_pos.reshape(chunks, tokens), k_cache.reshape(chunks, tokens * 128, 64), v_cache.reshape(chunks, tokens * 128, 64),
+            ids, w_query[0], w_key[0], w_value[0], w_out[0], attn_gain, mlp_gain, final_gain.astype(F32).reshape(8, 128), cos_t, sin_t, w_router[0].T,
             w_gate[0], w_up[0], w_down[0], tri,
         )
         out, k_new, v_new = step_call(args, chunks, tokens, tile_count)

time: 452 us -> 440 us (0.973)
  blocking collectives: 10.8 us -> 0 us
  Pallas kernels: 417 us -> 423 us
  local copies, waits for them, and re-layouts: 19 us -> 14.1 us
    all_gather x1 -> x0, blocking collectives: 10.8 us -> none  [device_fn(): lax.all_gather(expert_ids[0].reshape(chunks, tokens, 8), 'ep', axis=0, ti...]
    pallas_call x1, Pallas kernels: 417 us -> 423 us  [step_call(): pl.pallas_call(functools.partial(step_kernel, tile_count), out_shape=(jax...]
    unnamed x13 -> x9, local copies, waits for them, and re-layouts: 13.9 us -> 12.7 us
where the time goes in v4:
time: 440 us; the launch traced here: 439 us
  Pallas kernels  423 us (96%)
  local copies, waits for them, and re-layouts  14.1 us (3%)
    pallas_call x1, Pallas kernels, step_call(): pl.pallas_call(functools.partial(step_kernel, tile_count), out_shape=(jax...  423 us
    unnamed x9, local copies, waits for them, and re-layouts  12.7 us

profile of v4, /device:TPU:0, one launch (start us, length us, event | category | flops | bytes accessed | tf_op | source)
XLA Modules:
  0.0 439.3 jit_solution(732455717468784506)
XLA Ops:
  0.6 1.3 bitcast_convert_fusion.f_gain
  1.9 0.8 copy.23
  2.7 0.7 reshape.33.seq
  3.4 1.0 copy.24
  4.4 0.1 reshape_squeeze.3
  4.5 0.7 copy.27
  5.2 423.2 %decode_step.1 = (bf16[16,128,1024]{2,1,0:T(8,128)(2,1)}, bf16[16,128,8,64]{3,2,1,0:T(8,128)(2,1)}, bf16[16,128,8,64]{3,2,1,0:T(8,128)(2,1)}) custom-call(bf16[16,128,1024]{2,1,0:T(8,128)(2,1)} %bitcast.33, s32[16,128]{1,0:T(8,128)} %reshape.33.seq, bf16[16,16384,64]{2,1,0:T(8,128)(2,1)} %bitcast.1.k_cache, bf16[16,16384,64]{2,1,0:T(8,128)(2,1)} %bitcast.2.v_cache, ...), custom_call_target="tpu_custom_call" | custom-call | flops 199999995904 | bytes 200000000 | tf_op jit(solution)/shard_map/decode_step/pallas_call | solution.py:548
  428.4 0.0 copy-start.1
  428.5 5.2 %copy.31 = bf16[64,32,1024]{2,1,0:T(8,128)(2,1)} copy(bf16[64,32,1024]{2,1,0:T(8,128)(2,1)} %bitcast.28) | data formatting | bytes 8388608
  433.6 0.0 copy-done.1
  433.6 0.0 copy-start
  433.6 2.1 copy.32
  435.8 1.6 copy-done
  437.3 2.0 copy.33
Async XLA Ops:
  428.4 5.2 %copy-start.1 = (bf16[16,128,8,64]{3,2,1,0:T(8,128)(2,1)S(1)}, bf16[16,128,8,64]{3,2,1,0:T(8,128)(2,1)}, u32[]{:S(2)}) copy-start(bf16[16,128,8,64]{3,2,1,0:T(8,128)(2,1)} %get-tuple-element.7) | copy-start | bytes 6291460
  433.6 3.7 copy-start
